TPU v7x, 32 devices: a whole 2x2x4 slice. The times are simulated.
32 devices in a mesh: rows: 32 (over z, y, x, core).
Axes of the slice: x: 2, y: 2, z: 4, core: 2. Of those that a mesh axis runs over, the one named last changes fastest.
Arguments:
- coupling: float32 [128, 5, 128, 128], P('rows'), may hold values from -0.15 to 3.15, as said below
- columns: int32 [128, 5], replicated, may hold values from 0 to 63, as said below
- row_slots: int32 [64], replicated, may hold values from 0 to 127, as said below
Outputs:
- inverse_estimate: float32 [128, 5, 128, 128], P('rows')
Inputs may be any that keep to these rules, and one draw needn't show every extreme that they name: `coupling`: in every slot the diagonal entries of tile 0 are at least 0.3. `columns`: for a slot that holds block row r, entry 0 is r and the other 4 entries are distinct block rows (r + d) mod 64 with 1 <= |d| <= 3; entries of slots that hold no block row mean nothing. `row_slots`: device i owns slots i * 4 to (i + 1) * 4 - 1. Block rows are owned in order: device 0 holds the first ones, each device a contiguous run of rows in its first slots, at least 1 and at most 4 rows; some device holds 4.
All inputs are finite; a program needn't handle non-finite values.
Results may differ from a plain program's by a relative error of at most 0.0003.
Values sent between devices are 32-bit elements; how exact they have to be, the bound alone decides.
No kernel may reach another device: no remote copies, remote signals or barrier semaphores. Data moves between devices by JAX's collectives and lax.ppermute only.
A program may use at most 64 MiB of HBM per device.

v0:
```python
import jax
import jax.numpy as jnp
from jax import lax
from jax.sharding import PartitionSpec as P

BAND = 3


precise = lax.Precision.HIGHEST


def from_behind(value, axis, steps):
    count = lax.axis_size(axis)
    pairs = [(source, (source + steps) % count) for source in range(count)]
    return lax.ppermute(value, axis, pairs)


def ownership(row_slots, slot_count, devices):
    owners = row_slots // slot_count
    listed = jnp.arange(devices, dtype=jnp.int32)
    counts = jnp.sum((owners[None, :] == listed[:, None]).astype(jnp.int32), axis=1)
    starts = jnp.cumsum(counts) - counts
    return (counts, starts)


def held_rows(counts, starts, device, first_slot, length):
    position = first_slot + jnp.arange(length, dtype=jnp.int32)
    return jnp.where(position < counts[device], starts[device] + position, -1)


def upper_start(counts, device, limit, slot_count):
    return jnp.clip(counts[device] - limit, 0, slot_count - limit)


def locate(wanted, row_ids):
    matches = wanted[..., None] == row_ids
    return jnp.argmax(matches, axis=-1)


def start_iterate(coupling, inverse, column_inverse):
    identity = jnp.eye(coupling.shape[-1], dtype=coupling.dtype)
    leading = (jnp.arange(coupling.shape[1]) == 0).astype(coupling.dtype)
    diagonal_part = 2.0 * leading[None, :, None, None] * (inverse[:, None, :, None] * identity)
    return diagonal_part - inverse[:, None, :, None] * coupling * column_inverse[:, :, None, :]


def pattern_product(left, row_pool, row_ids, pool_columns, own_columns):

    def per_slot(operands):
        blocks, row_columns = operands
        located = locate(row_columns, row_ids)
        fetched = jnp.take(row_pool, located, axis=0)
        their_columns = jnp.take(pool_columns, located, axis=0)
        selector = (their_columns[:, :, None] == row_columns[None, None, :]).astype(row_pool.dtype)
        chosen = jnp.einsum("kab,kaqr->kbqr", selector, fetched, precision=precise)
        return jnp.einsum("kpq,kbqr->bpr", blocks, chosen, precision=precise)

    return lax.map(per_slot, (left, own_columns))


def fetch_inverse(inverse, counts, starts, own_index, devices):
    slot_count = inverse.shape[0]
    pieces = [inverse]
    row_ids = [held_rows(counts, starts, own_index, 0, slot_count)]
    for offset in range(1, BAND + 1):
        for heading in (1, -1):
            pieces.append(from_behind(inverse, "rows", heading * offset))
            source = (own_index - heading * offset) % devices
            row_ids.append(held_rows(counts, starts, source, 0, slot_count))
    return (jnp.concatenate(pieces, 0), jnp.concatenate(row_ids, 0))


def fetch_tiles(shard, counts, starts, own_index, devices):
    slot_count = shard.shape[0]
    limits = [min(slot_count, BAND - offset + 1) for offset in range(1, BAND + 1)]
    pieces = [shard]
    row_ids = [held_rows(counts, starts, own_index, 0, slot_count)]
    for offset in range(1, BAND + 1):
        limit = limits[offset - 1]
        for heading in (1, -1):
            source = (own_index - heading * offset) % devices
            if heading > 0:
                first_slot = upper_start(counts, source, limit, slot_count)
                own_first = upper_start(counts, own_index, limit, slot_count)
            else:
                first_slot = 0
                own_first = 0
            outgoing = lax.dynamic_slice_in_dim(shard, own_first, limit, 0)
            pieces.append(from_behind(outgoing, "rows", heading * offset))
            row_ids.append(held_rows(counts, starts, source, first_slot, limit))
    return (jnp.concatenate(pieces, 0), jnp.concatenate(row_ids, 0))


def shards(coupling, columns, row_slots):
    slot_count = coupling.shape[0]
    devices = lax.axis_size("rows")
    own_index = lax.axis_index("rows")
    counts, starts = ownership(row_slots, slot_count, devices)
    own_columns = lax.dynamic_slice_in_dim(columns, own_index * slot_count, slot_count, 0)
    own_rows = held_rows(counts, starts, own_index, 0, slot_count)
    occupied = own_rows >= 0
    inverse = 1.0 / jnp.diagonal(coupling[:, 0], axis1=1, axis2=2)
    inverse_pool, inverse_ids = fetch_inverse(inverse, counts, starts, own_index, devices)
    column_inverse = jnp.take(inverse_pool, locate(own_columns, inverse_ids), axis=0)
    first_iterate = start_iterate(coupling, inverse, column_inverse)
    row_pool, row_ids = fetch_tiles(first_iterate, counts, starts, own_index, devices)
    pool_columns = jnp.take(columns, jnp.take(row_slots, jnp.maximum(row_ids, 0)), axis=0)
    product = pattern_product(coupling, row_pool, row_ids, pool_columns, own_columns)
    product_pool = fetch_tiles(product, counts, starts, own_index, devices)[0]
    second_iterate = 2.0 * first_iterate - pattern_product(
        first_iterate, product_pool, row_ids, pool_columns, own_columns
    )
    return jnp.where(occupied[:, None, None, None], second_iterate, 0.0)


def solution(mesh):
    return jax.shard_map(
        shards,
        mesh=mesh,
        in_specs=(P("rows", None, None, None), P(), P()),
        out_specs=P("rows", None, None, None),
        check_vma=False,
    )
```

profile of v0, /device:TPU:0, one launch (start us, length us, event | category | flops | bytes accessed | tf_op | source)
XLA Modules:
  0.0 279.9 jit_solution(11326815432144722829)
XLA Ops:
  1.0 4.7 %copy.103 = f32[4,1,128,128]{0,3,2,1:T(8,128)} copy(f32[4,1,128,128]{3,2,1,0:T(8,128)S(1)} %slice.3) | data formatting | bytes 524288
  5.7 1.8 gather_fusion.4
  8.0 6.0 %collective-permute-start.1 = (f32[4,128]{0,1:T(8,128)S(1)}, f32[4,128]{0,1:T(8,128)S(1)}, u32[]{:S(2)}, u32[]{:S(2)}) collective-permute-start(f32[4,128]{0,1:T(8,128)S(1)} %divide_bitcast_fusion), channel_id=1, source_target_pairs={{0,31},{1,0},{2,1},{3,2},{4,3},{5,4},{6,5},{7,6},{8,7},{9,8},{10,9... | collective-permute-start | bytes 6152 | tf_op jit(solution)/shard_map/ppermute | solution.py:15
  14.0 5.6 %collective-permute-start.3 = (f32[4,128]{0,1:T(8,128)S(1)}, f32[4,128]{0,1:T(8,128)S(1)}, u32[]{:S(2)}, u32[]{:S(2)}) collective-permute-start(f32[4,128]{0,1:T(8,128)S(1)} %divide_bitcast_fusion), channel_id=1, source_target_pairs={{0,30},{1,31},{2,0},{3,1},{4,2},{5,3},{6,4},{7,5},{8,6},{9,7},{10,... | collective-permute-start | bytes 6152 | tf_op jit(solution)/shard_map/ppermute | solution.py:15
  21.1 1.3 compare_select_fusion.11
  22.4 1.2 compare_select_fusion.12
  23.6 1.2 compare_select_fusion.13
  24.9 1.2 compare_select_fusion.14
  27.3 1.3 compare_select_fusion.16
  28.6 1.3 broadcast_compare_fusion
  30.9 1.2 fusion.40
  37.7 1.3 fusion.41
  38.9 1.3 compare_select_fusion.8
  40.4 1.3 fusion.43
  45.1 4.5 %collective-permute-start.5 = (f32[4,128]{0,1:T(8,128)S(1)}, f32[4,128]{0,1:T(8,128)S(1)}, u32[]{:S(2)}, u32[]{:S(2)}) collective-permute-start(f32[4,128]{0,1:T(8,128)S(1)} %divide_bitcast_fusion), channel_id=1, source_target_pairs={{0,29},{1,30},{2,31},{3,0},{4,1},{5,2},{6,3},{7,4},{8,5},{9,6},{10... | collective-permute-start | bytes 6152 | tf_op jit(solution)/shard_map/ppermute | solution.py:15
  49.6 1.3 compare_select_fusion.10
  53.7 1.4 constant_dynamic-update-slice_fusion.8
  55.1 1.6 fusion.37
  56.7 5.4 %collective-permute-start.7 = (f32[3,5,128,128]{3,2,1,0:T(8,128)}, f32[3,5,128,128]{3,2,1,0:T(8,128)}, u32[]{:S(2)}, u32[]{:S(2)}) collective-permute-start(f32[3,5,128,128]{3,2,1,0:T(8,128)} %get-tuple-element.185), channel_id=1, source_target_pairs={{0,31},{1,0},{2,1},{3,2},{4,3},{5,4},{6,5},{7,6},{8,7},{9,8},{10,9... | collective-permute-start | bytes 2949128 | tf_op jit(solution)/shard_map/ppermute | solution.py:15
  63.8 5.6 %collective-permute-start.9 = (f32[2,5,128,128]{3,2,1,0:T(8,128)}, f32[2,5,128,128]{3,2,1,0:T(8,128)S(1)}, u32[]{:S(2)}, u32[]{:S(2)}) collective-permute-start(f32[2,5,128,128]{3,2,1,0:T(8,128)} %get-tuple-element.183), channel_id=1, source_target_pairs={{0,30},{1,31},{2,0},{3,1},{4,2},{5,3},{6,4},{7,5},{8,6},{9,7},{10,... | collective-permute-start | bytes 1966088 | tf_op jit(solution)/shard_map/ppermute | solution.py:15
  70.3 7.6 %collective-permute-done.6 = f32[3,5,128,128]{3,2,1,0:T(8,128)} collective-permute-done((f32[3,5,128,128]{3,2,1,0:T(8,128)}, f32[3,5,128,128]{3,2,1,0:T(8,128)}, u32[]{:S(2)}, u32[]{:S(2)}) %collective-permute-start.6) | collective-permute-done | bytes 983072 | tf_op jit(solution)/shard_map/ppermute | solution.py:15
  77.9 3.0 %collective-permute-start.11 = (f32[1,5,128,128]{3,2,1,0:T(8,128)S(1)}, f32[1,5,128,128]{3,2,1,0:T(8,128)S(1)}, u32[]{:S(2)}, u32[]{:S(2)}) collective-permute-start(f32[1,5,128,128]{3,2,1,0:T(8,128)S(1)} %get-tuple-element.181), channel_id=1, source_target_pairs={{0,29},{1,30},{2,31},{3,0},{4,1},{5,2},{6,3},{7,4},{8,5},{9,6},{10... | collective-permute-start | bytes 983048 | tf_op jit(solution)/shard_map/ppermute | solution.py:15
  80.9 2.3 constant_dynamic-update-slice_fusion.7
  83.2 2.3 constant_dynamic-update-slice_fusion.6
  85.5 14.3 %collective-permute-done.8 = f32[2,5,128,128]{3,2,1,0:T(8,128)} collective-permute-done((f32[2,5,128,128]{3,2,1,0:T(8,128)}, f32[2,5,128,128]{3,2,1,0:T(8,128)}, u32[]{:S(2)}, u32[]{:S(2)}) %collective-permute-start.8) | collective-permute-done | bytes 655392 | tf_op jit(solution)/shard_map/ppermute | solution.py:15
  99.8 2.0 constant_dynamic-update-slice_fusion.5
  101.8 7.9 %collective-permute-done.9 = f32[2,5,128,128]{3,2,1,0:T(8,128)S(1)} collective-permute-done((f32[2,5,128,128]{3,2,1,0:T(8,128)}, f32[2,5,128,128]{3,2,1,0:T(8,128)S(1)}, u32[]{:S(2)}, u32[]{:S(2)}) %collective-permute-start.9) | collective-permute-done | bytes 655392 | tf_op jit(solution)/shard_map/ppermute | solution.py:15
  111.3 2.1 collective-permute-done.11
  115.4 47.4 %while.20 = (s32[]{:T(128)}, f32[4,5,128,128]{3,2,1,0:T(8,128)}, s32[4,5]{1,0:T(4,128)S(1)}, s32[16]{0:T(128)S(1)}, s32[16,5]{1,0:T(8,128)S(1)}, /*index=5*/f32[...) while((s32[]{:T(128)}, f32[4,5,128,128]{3,2,1,0:T(8,128)}, ...), condition=%wide.region_5.8_spmd, body=%wide.region_3.7_spmd.sunk | while | flops 654132992 | bytes 18683808 | solution.py:58
  116.1 3.1 %gather_fusion = f32[5,5,128,128]{3,2,1,0:T(8,128)S(1)} fusion(f32[16,5,128,128]{3,2,1,0:T(8,128)} %get-tuple-element.319, s32[1024]{0:T(1024)S(1)} %pad_clamp_fusion.7), kind=kCustom, calls=%fused_computation.1.clone.clone.1 | custom fusion | bytes 3276820 | tf_op jit(solution)/shard_map/while/body/eval_jaxpr/jit(_take)/gather | solution.py:52
  120.2 2.2 fusion.63
  122.4 3.9 %fusion.64 = f32[1,5,128,128]{2,3,1,0:T(8,128)S(1)} fusion(f32[5,5,128,128]{3,1,2,0:T(8,128)S(1)} %fusion.63, f32[4,5,128,128]{3,2,1,0:T(8,128)} %get-tuple-element.356, s32[]{:T(128)} %get-tuple-element.306), kind=kOutput, calls=%fused_computation.12.clone.1 | convolution fusion | flops 629145600 | bytes 2294272 | tf_op jit(solution)/shard_map/while/body/eval_jaxpr/kpq,kbqr->bpr/dot_general | solution.py:56
  128.0 3.1 %gather_fusion = f32[5,5,128,128]{3,2,1,0:T(8,128)S(1)} fusion(f32[16,5,128,128]{3,2,1,0:T(8,128)} %get-tuple-element.319, s32[1024]{0:T(1024)S(1)} %pad_clamp_fusion.7), kind=kCustom, calls=%fused_computation.1.clone.clone.1 | custom fusion | bytes 3276820 | tf_op jit(solution)/shard_map/while/body/eval_jaxpr/jit(_take)/gather | solution.py:52
  132.0 2.2 fusion.63
  134.3 3.9 %fusion.64 = f32[1,5,128,128]{2,3,1,0:T(8,128)S(1)} fusion(f32[5,5,128,128]{3,1,2,0:T(8,128)S(1)} %fusion.63, f32[4,5,128,128]{3,2,1,0:T(8,128)} %get-tuple-element.356, s32[]{:T(128)} %get-tuple-element.306), kind=kOutput, calls=%fused_computation.12.clone.1 | convolution fusion | flops 629145600 | bytes 2294272 | tf_op jit(solution)/shard_map/while/body/eval_jaxpr/kpq,kbqr->bpr/dot_general | solution.py:56
  139.8 3.1 %gather_fusion = f32[5,5,128,128]{3,2,1,0:T(8,128)S(1)} fusion(f32[16,5,128,128]{3,2,1,0:T(8,128)} %get-tuple-element.319, s32[1024]{0:T(1024)S(1)} %pad_clamp_fusion.7), kind=kCustom, calls=%fused_computation.1.clone.clone.1 | custom fusion | bytes 3276820 | tf_op jit(solution)/shard_map/while/body/eval_jaxpr/jit(_take)/gather | solution.py:52
  143.9 2.2 fusion.63
  146.1 3.9 %fusion.64 = f32[1,5,128,128]{2,3,1,0:T(8,128)S(1)} fusion(f32[5,5,128,128]{3,1,2,0:T(8,128)S(1)} %fusion.63, f32[4,5,128,128]{3,2,1,0:T(8,128)} %get-tuple-element.356, s32[]{:T(128)} %get-tuple-element.306), kind=kOutput, calls=%fused_computation.12.clone.1 | convolution fusion | flops 629145600 | bytes 2294272 | tf_op jit(solution)/shard_map/while/body/eval_jaxpr/kpq,kbqr->bpr/dot_general | solution.py:56
  151.7 3.1 %gather_fusion = f32[5,5,128,128]{3,2,1,0:T(8,128)S(1)} fusion(f32[16,5,128,128]{3,2,1,0:T(8,128)} %get-tuple-element.319, s32[1024]{0:T(1024)S(1)} %pad_clamp_fusion.7), kind=kCustom, calls=%fused_computation.1.clone.clone.1 | custom fusion | bytes 3276820 | tf_op jit(solution)/shard_map/while/body/eval_jaxpr/jit(_take)/gather | solution.py:52
  155.8 2.2 fusion.63
  158.0 3.9 %fusion.64 = f32[1,5,128,128]{2,3,1,0:T(8,128)S(1)} fusion(f32[5,5,128,128]{3,1,2,0:T(8,128)S(1)} %fusion.63, f32[4,5,128,128]{3,2,1,0:T(8,128)} %get-tuple-element.356, s32[]{:T(128)} %get-tuple-element.306), kind=kOutput, calls=%fused_computation.12.clone.1 | convolution fusion | flops 629145600 | bytes 2294272 | tf_op jit(solution)/shard_map/while/body/eval_jaxpr/kpq,kbqr->bpr/dot_general | solution.py:56
  162.8 1.8 fusion.34
  165.5 4.9 %collective-permute-start.13 = (f32[3,5,128,128]{3,2,1,0:T(8,128)S(1)}, f32[3,5,128,128]{3,2,1,0:T(8,128)S(1)}, u32[]{:S(2)}, u32[]{:S(2)}) collective-permute-start(f32[3,5,128,128]{3,2,1,0:T(8,128)S(1)} %get-tuple-element.179), channel_id=1, source_target_pairs={{0,31},{1,0},{2,1},{3,2},{4,3},{5,4},{6,5},{7,6},{8,7},{9,8},{10,9... | collective-permute-start | bytes 2949128 | tf_op jit(solution)/shard_map/ppermute | solution.py:15
  170.6 5.6 %collective-permute-start.15 = (f32[2,5,128,128]{3,2,1,0:T(8,128)S(1)}, f32[2,5,128,128]{3,2,1,0:T(8,128)S(1)}, u32[]{:S(2)}, u32[]{:S(2)}) collective-permute-start(f32[2,5,128,128]{3,2,1,0:T(8,128)S(1)} %get-tuple-element.177), channel_id=1, source_target_pairs={{0,30},{1,31},{2,0},{3,1},{4,2},{5,3},{6,4},{7,5},{8,6},{9,7},{10,... | collective-permute-start | bytes 1966088 | tf_op jit(solution)/shard_map/ppermute | solution.py:15
  176.4 13.7 %collective-permute-done.12 = f32[3,5,128,128]{3,2,1,0:T(8,128)S(1)} collective-permute-done((f32[3,5,128,128]{3,2,1,0:T(8,128)S(1)}, f32[3,5,128,128]{3,2,1,0:T(8,128)S(1)}, u32[]{:S(2)}, u32[]{:S(2)}) %collective-permute-start.12) | collective-permute-done | bytes 983072 | tf_op jit(solution)/shard_map/ppermute | solution.py:15
  190.3 17.5 %collective-permute-done.14 = f32[2,5,128,128]{3,2,1,0:T(8,128)S(1)} collective-permute-done((f32[2,5,128,128]{3,2,1,0:T(8,128)S(1)}, f32[2,5,128,128]{3,2,1,0:T(8,128)S(1)}, u32[]{:S(2)}, u32[]{:S(2)}) %collective-permute-start.14) | collective-permute-done | bytes 655392 | tf_op jit(solution)/shard_map/ppermute | solution.py:15
  207.9 14.6 %collective-permute-done.15 = f32[2,5,128,128]{3,2,1,0:T(8,128)S(1)} collective-permute-done((f32[2,5,128,128]{3,2,1,0:T(8,128)S(1)}, f32[2,5,128,128]{3,2,1,0:T(8,128)S(1)}, u32[]{:S(2)}, u32[]{:S(2)}) %collective-permute-start.15) | collective-permute-done | bytes 655392 | tf_op jit(solution)/shard_map/ppermute | solution.py:15
  222.6 4.6 %collective-permute-done.17 = f32[1,5,128,128]{3,2,1,0:T(8,128)S(1)} collective-permute-done((f32[1,5,128,128]{3,2,1,0:T(8,128)S(1)}, f32[1,5,128,128]{3,2,1,0:T(8,128)S(1)}, u32[]{:S(2)}, u32[]{:S(2)}) %collective-permute-start.17) | collective-permute-done | bytes 327712 | tf_op jit(solution)/shard_map/ppermute | solution.py:15
  227.2 1.3 broadcast.334.clone2
  228.6 1.4 copy-done.3
  229.9 47.0 %while.21 = (s32[]{:T(128)}, f32[4,5,128,128]{3,2,1,0:T(8,128)}, s32[4,5]{1,0:T(4,128)S(1)}, s32[16]{0:T(128)S(1)}, s32[16,5]{1,0:T(8,128)S(1)}, /*index=5*/f32[...) while((s32[]{:T(128)}, f32[4,5,128,128]{3,2,1,0:T(8,128)}, s32[4,5]{1,0:T(4,128)S(1)}, ...), condition=%wide.region_8.11_spmd, body=%wide.region_6.10_spmd.sunk | while | flops 654132992 | bytes 13440893 | solution.py:58
  230.7 3.1 %gather_fusion.2 = f32[5,5,128,128]{3,2,1,0:T(8,128)S(1)} fusion(f32[16,5,128,128]{3,2,1,0:T(8,128)} %get-tuple-element.343, s32[1024]{0:T(1024)S(1)} %pad_clamp_fusion.8), kind=kCustom, calls=%fused_computation.3.clone.clone.1 | custom fusion | bytes 3276820 | tf_op jit(solution)/shard_map/while/body/eval_jaxpr/jit(_take)/gather | solution.py:52
  234.7 2.2 fusion.70
  236.9 3.8 %fusion.71 = f32[1,5,128,128]{2,3,1,0:T(8,128)S(1)} fusion(f32[5,5,128,128]{3,1,2,0:T(8,128)S(1)} %fusion.70, f32[4,5,128,128]{3,2,1,0:T(8,128)} %get-tuple-element.344, s32[]{:T(128)} %get-tuple-element.330), kind=kOutput, calls=%fused_computation.33.clone.1 | convolution fusion | flops 629145600 | bytes 2294272 | tf_op jit(solution)/shard_map/while/body/eval_jaxpr/kpq,kbqr->bpr/dot_general | solution.py:56
  242.4 3.1 %gather_fusion.2 = f32[5,5,128,128]{3,2,1,0:T(8,128)S(1)} fusion(f32[16,5,128,128]{3,2,1,0:T(8,128)} %get-tuple-element.343, s32[1024]{0:T(1024)S(1)} %pad_clamp_fusion.8), kind=kCustom, calls=%fused_computation.3.clone.clone.1 | custom fusion | bytes 3276820 | tf_op jit(solution)/shard_map/while/body/eval_jaxpr/jit(_take)/gather | solution.py:52
  246.5 2.2 fusion.70
  248.7 3.8 %fusion.71 = f32[1,5,128,128]{2,3,1,0:T(8,128)S(1)} fusion(f32[5,5,128,128]{3,1,2,0:T(8,128)S(1)} %fusion.70, f32[4,5,128,128]{3,2,1,0:T(8,128)} %get-tuple-element.344, s32[]{:T(128)} %get-tuple-element.330), kind=kOutput, calls=%fused_computation.33.clone.1 | convolution fusion | flops 629145600 | bytes 2294272 | tf_op jit(solution)/shard_map/while/body/eval_jaxpr/kpq,kbqr->bpr/dot_general | solution.py:56
  254.1 3.1 %gather_fusion.2 = f32[5,5,128,128]{3,2,1,0:T(8,128)S(1)} fusion(f32[16,5,128,128]{3,2,1,0:T(8,128)} %get-tuple-element.343, s32[1024]{0:T(1024)S(1)} %pad_clamp_fusion.8), kind=kCustom, calls=%fused_computation.3.clone.clone.1 | custom fusion | bytes 3276820 | tf_op jit(solution)/shard_map/while/body/eval_jaxpr/jit(_take)/gather | solution.py:52
  258.2 2.2 fusion.70
  260.4 3.8 %fusion.71 = f32[1,5,128,128]{2,3,1,0:T(8,128)S(1)} fusion(f32[5,5,128,128]{3,1,2,0:T(8,128)S(1)} %fusion.70, f32[4,5,128,128]{3,2,1,0:T(8,128)} %get-tuple-element.344, s32[]{:T(128)} %get-tuple-element.330), kind=kOutput, calls=%fused_computation.33.clone.1 | convolution fusion | flops 629145600 | bytes 2294272 | tf_op jit(solution)/shard_map/while/body/eval_jaxpr/kpq,kbqr->bpr/dot_general | solution.py:56
  265.9 3.1 %gather_fusion.2 = f32[5,5,128,128]{3,2,1,0:T(8,128)S(1)} fusion(f32[16,5,128,128]{3,2,1,0:T(8,128)} %get-tuple-element.343, s32[1024]{0:T(1024)S(1)} %pad_clamp_fusion.8), kind=kCustom, calls=%fused_computation.3.clone.clone.1 | custom fusion | bytes 3276820 | tf_op jit(solution)/shard_map/while/body/eval_jaxpr/jit(_take)/gather | solution.py:52
  269.9 2.2 fusion.70
  272.2 3.8 %fusion.71 = f32[1,5,128,128]{2,3,1,0:T(8,128)S(1)} fusion(f32[5,5,128,128]{3,1,2,0:T(8,128)S(1)} %fusion.70, f32[4,5,128,128]{3,2,1,0:T(8,128)} %get-tuple-element.344, s32[]{:T(128)} %get-tuple-element.330), kind=kOutput, calls=%fused_computation.33.clone.1 | convolution fusion | flops 629145600 | bytes 2294272 | tf_op jit(solution)/shard_map/while/body/eval_jaxpr/kpq,kbqr->bpr/dot_general | solution.py:56
  276.9 3.0 %subtract_select_fusion = f32[4,5,128,128]{3,2,1,0:T(8,128)} fusion(f32[4,5,128,128]{3,2,1,0:T(8,128)} %get-tuple-element.86, f32[4,5,128,128]{3,2,1,0:T(8,128)} %get-tuple-element.346, pred[4]{0:T(512)(128)(4,1)S(1)} %get-tuple-element.171), kind=kLoop, calls=%fused_computation.50 | loop fusion | flops 983040 | bytes 3932164 | tf_op jit(solution)/shard_map/jit(_where)/select_n | solution.py:113
  (183 shorter events, 38.7 us)
Async XLA Ops:
  1.0 18.7 %copy-start = (s32[64]{0:T(128)S(1)}, s32[64]{0:T(128)}, u32[]{:S(2)}) copy-start(s32[64]{0:T(128)} %param.13) | copy-start | bytes 772
  1.0 19.1 %copy-start.6 = (s32[128,5]{0,1:T(8,128)S(1)}, s32[128,5]{0,1:T(8,128)}, u32[]{:S(2)}) copy-start(s32[128,5]{0,1:T(8,128)} %param.12) | copy-start | bytes 7684
  5.7 48.0 %copy-start.4 = (f32[4,5,128,128]{3,2,1,0:T(8,128)S(1)}, f32[4,5,128,128]{3,2,1,0:T(8,128)}, u32[]{:S(2)}) copy-start(f32[4,5,128,128]{3,2,1,0:T(8,128)} %param.11) | copy-start | bytes 3932164
  7.5 37.6 %collective-permute-start = (f32[4,128]{0,1:T(8,128)S(1)}, f32[4,128]{0,1:T(8,128)S(1)}, u32[]{:S(2)}, u32[]{:S(2)}) collective-permute-start(f32[4,128]{0,1:T(8,128)S(1)} %divide_bitcast_fusion), channel_id=1, source_target_pairs={{0,1},{1,2},{2,3},{3,4},{4,5},{5,6},{6,7},{7,8},{8,9},{9,10},{10,1... | collective-permute-start | bytes 6152 | tf_op jit(solution)/shard_map/ppermute | solution.py:15
  8.0 44.5 %collective-permute-start.1 = (f32[4,128]{0,1:T(8,128)S(1)}, f32[4,128]{0,1:T(8,128)S(1)}, u32[]{:S(2)}, u32[]{:S(2)}) collective-permute-start(f32[4,128]{0,1:T(8,128)S(1)} %divide_bitcast_fusion), channel_id=1, source_target_pairs={{0,31},{1,0},{2,1},{3,2},{4,3},{5,4},{6,5},{7,6},{8,7},{9,8},{10,9... | collective-permute-start | bytes 6152 | tf_op jit(solution)/shard_map/ppermute | solution.py:15
  14.0 38.6 %collective-permute-start.2 = (f32[4,128]{0,1:T(8,128)S(1)}, f32[4,128]{0,1:T(8,128)S(1)}, u32[]{:S(2)}, u32[]{:S(2)}) collective-permute-start(f32[4,128]{0,1:T(8,128)S(1)} %divide_bitcast_fusion), channel_id=1, source_target_pairs={{0,2},{1,3},{2,4},{3,5},{4,6},{5,7},{6,8},{7,9},{8,10},{9,11},{10,... | collective-permute-start | bytes 6152 | tf_op jit(solution)/shard_map/ppermute | solution.py:15
  14.0 38.6 %collective-permute-start.3 = (f32[4,128]{0,1:T(8,128)S(1)}, f32[4,128]{0,1:T(8,128)S(1)}, u32[]{:S(2)}, u32[]{:S(2)}) collective-permute-start(f32[4,128]{0,1:T(8,128)S(1)} %divide_bitcast_fusion), channel_id=1, source_target_pairs={{0,30},{1,31},{2,0},{3,1},{4,2},{5,3},{6,4},{7,5},{8,6},{9,7},{10,... | collective-permute-start | bytes 6152 | tf_op jit(solution)/shard_map/ppermute | solution.py:15
  19.6 33.1 %collective-permute-start.4 = (f32[4,128]{0,1:T(8,128)S(1)}, f32[4,128]{0,1:T(8,128)S(1)}, u32[]{:S(2)}, u32[]{:S(2)}) collective-permute-start(f32[4,128]{0,1:T(8,128)S(1)} %divide_bitcast_fusion), channel_id=1, source_target_pairs={{0,3},{1,4},{2,5},{3,6},{4,7},{5,8},{6,9},{7,10},{8,11},{9,12},{10... | collective-permute-start | bytes 6152 | tf_op jit(solution)/shard_map/ppermute | solution.py:15
  45.1 7.7 %collective-permute-start.5 = (f32[4,128]{0,1:T(8,128)S(1)}, f32[4,128]{0,1:T(8,128)S(1)}, u32[]{:S(2)}, u32[]{:S(2)}) collective-permute-start(f32[4,128]{0,1:T(8,128)S(1)} %divide_bitcast_fusion), channel_id=1, source_target_pairs={{0,29},{1,30},{2,31},{3,0},{4,1},{5,2},{6,3},{7,4},{8,5},{9,6},{10... | collective-permute-start | bytes 6152 | tf_op jit(solution)/shard_map/ppermute | solution.py:15
  55.1 15.1 %copy-start.1 = (f32[4,5,128,128]{3,2,1,0:T(8,128)}, f32[4,5,128,128]{3,2,1,0:T(8,128)S(1)}, u32[]{:S(2)}) copy-start(f32[4,5,128,128]{3,2,1,0:T(8,128)S(1)} %get-tuple-element.328) | copy-start | bytes 3932164
  56.7 21.2 %collective-permute-start.6 = (f32[3,5,128,128]{3,2,1,0:T(8,128)}, f32[3,5,128,128]{3,2,1,0:T(8,128)}, u32[]{:S(2)}, u32[]{:S(2)}) collective-permute-start(f32[3,5,128,128]{3,2,1,0:T(8,128)} %get-tuple-element.186), channel_id=1, source_target_pairs={{0,1},{1,2},{2,3},{3,4},{4,5},{5,6},{6,7},{7,8},{8,9},{9,10},{10,1... | collective-permute-start | bytes 2949128 | tf_op jit(solution)/shard_map/ppermute | solution.py:15
  56.7 26.5 %collective-permute-start.7 = (f32[3,5,128,128]{3,2,1,0:T(8,128)}, f32[3,5,128,128]{3,2,1,0:T(8,128)}, u32[]{:S(2)}, u32[]{:S(2)}) collective-permute-start(f32[3,5,128,128]{3,2,1,0:T(8,128)} %get-tuple-element.185), channel_id=1, source_target_pairs={{0,31},{1,0},{2,1},{3,2},{4,3},{5,4},{6,5},{7,6},{8,7},{9,8},{10,9... | collective-permute-start | bytes 2949128 | tf_op jit(solution)/shard_map/ppermute | solution.py:15
  63.8 36.0 %collective-permute-start.8 = (f32[2,5,128,128]{3,2,1,0:T(8,128)}, f32[2,5,128,128]{3,2,1,0:T(8,128)}, u32[]{:S(2)}, u32[]{:S(2)}) collective-permute-start(f32[2,5,128,128]{3,2,1,0:T(8,128)} %get-tuple-element.184), channel_id=1, source_target_pairs={{0,2},{1,3},{2,4},{3,5},{4,6},{5,7},{6,8},{7,9},{8,10},{9,11},{10,... | collective-permute-start | bytes 1966088 | tf_op jit(solution)/shard_map/ppermute | solution.py:15
  63.8 45.9 %collective-permute-start.9 = (f32[2,5,128,128]{3,2,1,0:T(8,128)}, f32[2,5,128,128]{3,2,1,0:T(8,128)S(1)}, u32[]{:S(2)}, u32[]{:S(2)}) collective-permute-start(f32[2,5,128,128]{3,2,1,0:T(8,128)} %get-tuple-element.183), channel_id=1, source_target_pairs={{0,30},{1,31},{2,0},{3,1},{4,2},{5,3},{6,4},{7,5},{8,6},{9,7},{10,... | collective-permute-start | bytes 1966088 | tf_op jit(solution)/shard_map/ppermute | solution.py:15
  70.3 40.3 %collective-permute-start.10 = (f32[1,5,128,128]{3,2,1,0:T(8,128)S(1)}, f32[1,5,128,128]{3,2,1,0:T(8,128)S(1)}, u32[]{:S(2)}, u32[]{:S(2)}) collective-permute-start(f32[1,5,128,128]{3,2,1,0:T(8,128)S(1)} %get-tuple-element.182), channel_id=1, source_target_pairs={{0,3},{1,4},{2,5},{3,6},{4,7},{5,8},{6,9},{7,10},{8,11},{9,12},{10... | collective-permute-start | bytes 983048 | tf_op jit(solution)/shard_map/ppermute | solution.py:15
  77.9 35.5 %collective-permute-start.11 = (f32[1,5,128,128]{3,2,1,0:T(8,128)S(1)}, f32[1,5,128,128]{3,2,1,0:T(8,128)S(1)}, u32[]{:S(2)}, u32[]{:S(2)}) collective-permute-start(f32[1,5,128,128]{3,2,1,0:T(8,128)S(1)} %get-tuple-element.181), channel_id=1, source_target_pairs={{0,29},{1,30},{2,31},{3,0},{4,1},{5,2},{6,3},{7,4},{8,5},{9,6},{10... | collective-permute-start | bytes 983048 | tf_op jit(solution)/shard_map/ppermute | solution.py:15
  122.4 4.8 %copy-start.5 = (f32[4,5,128,128]{3,2,1,0:T(8,128)S(1)}, f32[4,5,128,128]{3,2,1,0:T(8,128)}, u32[]{:S(2)}) copy-start(f32[4,5,128,128]{3,2,1,0:T(8,128)} %get-tuple-element.356) | copy-start | bytes 3932164 | tf_op jit(solution)/shard_map/while
  134.3 4.8 %copy-start.5 = (f32[4,5,128,128]{3,2,1,0:T(8,128)S(1)}, f32[4,5,128,128]{3,2,1,0:T(8,128)}, u32[]{:S(2)}) copy-start(f32[4,5,128,128]{3,2,1,0:T(8,128)} %get-tuple-element.356) | copy-start | bytes 3932164 | tf_op jit(solution)/shard_map/while
  146.1 4.8 %copy-start.5 = (f32[4,5,128,128]{3,2,1,0:T(8,128)S(1)}, f32[4,5,128,128]{3,2,1,0:T(8,128)}, u32[]{:S(2)}) copy-start(f32[4,5,128,128]{3,2,1,0:T(8,128)} %get-tuple-element.356) | copy-start | bytes 3932164 | tf_op jit(solution)/shard_map/while
  158.0 4.8 %copy-start.5 = (f32[4,5,128,128]{3,2,1,0:T(8,128)S(1)}, f32[4,5,128,128]{3,2,1,0:T(8,128)}, u32[]{:S(2)}) copy-start(f32[4,5,128,128]{3,2,1,0:T(8,128)} %get-tuple-element.356) | copy-start | bytes 3932164 | tf_op jit(solution)/shard_map/while
  162.8 7.6 %copy-start.2 = (f32[4,5,128,128]{3,2,1,0:T(8,128)S(1)}, f32[4,5,128,128]{3,2,1,0:T(8,128)}, u32[]{:S(2)}) copy-start(f32[4,5,128,128]{3,2,1,0:T(8,128)} %get-tuple-element.349) | copy-start | bytes 3932164
  164.6 25.5 %collective-permute-start.12 = (f32[3,5,128,128]{3,2,1,0:T(8,128)S(1)}, f32[3,5,128,128]{3,2,1,0:T(8,128)S(1)}, u32[]{:S(2)}, u32[]{:S(2)}) collective-permute-start(f32[3,5,128,128]{3,2,1,0:T(8,128)S(1)} %get-tuple-element.180), channel_id=1, source_target_pairs={{0,1},{1,2},{2,3},{3,4},{4,5},{5,6},{6,7},{7,8},{8,9},{9,10},{10,1... | collective-permute-start | bytes 2949128 | tf_op jit(solution)/shard_map/ppermute | solution.py:15
  165.5 24.7 %collective-permute-start.13 = (f32[3,5,128,128]{3,2,1,0:T(8,128)S(1)}, f32[3,5,128,128]{3,2,1,0:T(8,128)S(1)}, u32[]{:S(2)}, u32[]{:S(2)}) collective-permute-start(f32[3,5,128,128]{3,2,1,0:T(8,128)S(1)} %get-tuple-element.179), channel_id=1, source_target_pairs={{0,31},{1,0},{2,1},{3,2},{4,3},{5,4},{6,5},{7,6},{8,7},{9,8},{10,9... | collective-permute-start | bytes 2949128 | tf_op jit(solution)/shard_map/ppermute | solution.py:15
  170.5 37.3 %collective-permute-start.14 = (f32[2,5,128,128]{3,2,1,0:T(8,128)S(1)}, f32[2,5,128,128]{3,2,1,0:T(8,128)S(1)}, u32[]{:S(2)}, u32[]{:S(2)}) collective-permute-start(f32[2,5,128,128]{3,2,1,0:T(8,128)S(1)} %get-tuple-element.178), channel_id=1, source_target_pairs={{0,2},{1,3},{2,4},{3,5},{4,6},{5,7},{6,8},{7,9},{8,10},{9,11},{10,... | collective-permute-start | bytes 1966088 | tf_op jit(solution)/shard_map/ppermute | solution.py:15
  170.6 51.9 %collective-permute-start.15 = (f32[2,5,128,128]{3,2,1,0:T(8,128)S(1)}, f32[2,5,128,128]{3,2,1,0:T(8,128)S(1)}, u32[]{:S(2)}, u32[]{:S(2)}) collective-permute-start(f32[2,5,128,128]{3,2,1,0:T(8,128)S(1)} %get-tuple-element.177), channel_id=1, source_target_pairs={{0,30},{1,31},{2,0},{3,1},{4,2},{5,3},{6,4},{7,5},{8,6},{9,7},{10,... | collective-permute-start | bytes 1966088 | tf_op jit(solution)/shard_map/ppermute | solution.py:15
  176.2 46.3 %collective-permute-start.16 = (f32[1,5,128,128]{3,2,1,0:T(8,128)S(1)}, f32[1,5,128,128]{3,2,1,0:T(8,128)S(1)}, u32[]{:S(2)}, u32[]{:S(2)}) collective-permute-start(f32[1,5,128,128]{3,2,1,0:T(8,128)S(1)} %get-tuple-element.176), channel_id=1, source_target_pairs={{0,3},{1,4},{2,5},{3,6},{4,7},{5,8},{6,9},{7,10},{8,11},{9,12},{10... | collective-permute-start | bytes 983048 | tf_op jit(solution)/shard_map/ppermute | solution.py:15
  190.1 37.1 %collective-permute-start.17 = (f32[1,5,128,128]{3,2,1,0:T(8,128)S(1)}, f32[1,5,128,128]{3,2,1,0:T(8,128)S(1)}, u32[]{:S(2)}, u32[]{:S(2)}) collective-permute-start(f32[1,5,128,128]{3,2,1,0:T(8,128)S(1)} %get-tuple-element.175), channel_id=1, source_target_pairs={{0,29},{1,30},{2,31},{3,0},{4,1},{5,2},{6,3},{7,4},{8,5},{9,6},{10... | collective-permute-start | bytes 983048 | tf_op jit(solution)/shard_map/ppermute | solution.py:15
  227.2 2.7 copy-start.3
where the time goes:
time: 281 us; the launch traced here: 280 us
  waiting for transfers between devices  82.4 us (29%)
  local copies, waits for them, and re-layouts  66.3 us (24%)
  matrix products  48.4 us (17%)
  starting transfers between devices  42.2 us (15%)
  other arithmetic  33.3 us (12%)
  between operations  6.88 us (2%)
    ppermute x18, waiting for transfers between devices, from_behind(): return lax.ppermute(value, axis, pairs)  82.4 us
    ppermute x18, starting transfers between devices, from_behind(): return lax.ppermute(value, axis, pairs)  42.2 us
    dot_general x8, matrix products, per_slot(): return jnp.einsum('kpq,kbqr->bpr', blocks, chosen, precision=precise)  30.7 us
    gather x8, local copies, waits for them, and re-layouts, per_slot(): fetched = jnp.take(row_pool, located, axis=0)  25.1 us
    dot_general x8, matrix products, per_slot(): chosen = jnp.einsum('kab,kaqr->kbqr', selector, fetched, precision=precise)  17.7 us
    unnamed x25, local copies, waits for them, and re-layouts  14.7 us
    select_n x10, other arithmetic, held_rows(): return jnp.where(position < counts[device], starts[device] + position, -1)  12.4 us
    dynamic_update_slice x16, local copies, waits for them, and re-layouts, pattern_product(): return lax.map(per_slot, (left, own_columns))  7.33 us
  transfers between devices with their start and end apart: 18, of which 8 were waited for; matrix products, arithmetic and copies ran while one was open for 12% of the time, Pallas kernels for 0%

commit v1 on v0

v1 whole, which is shorter than its diff:
```python
import jax
import jax.numpy as jnp
from jax import lax
from jax.experimental import pallas as pl
from jax.experimental.pallas import tpu as pltpu
from jax.sharding import PartitionSpec as P


BAND = 3
REACH = 2 * BAND
GROUP = 2
SHIFTS = 3
STARTS = 2 * SHIFTS + 4

FAR = [(d, step) for d in range(BAND + 1, REACH + 1) for step in range(d - BAND, BAND + 1)]


def far_slots(shift):
    return [(d, step) for d, step in FAR if d > GROUP * (shift - 1)]


def group_starts(row_slots, slot_count, devices, own_index):
    groups = devices // GROUP
    group = own_index // GROUP
    steps = jnp.arange(-SHIFTS, SHIFTS + 2, dtype=jnp.int32)
    wanted = group + steps
    turns = jnp.floor_divide(wanted, groups)
    firsts = jnp.concatenate([(wanted - turns * groups) * GROUP, group[None] * GROUP + 1])
    turns = jnp.concatenate([turns, jnp.zeros((1,), jnp.int32)])
    below = (row_slots[None, :] < (firsts * slot_count)[:, None]).astype(jnp.int32)
    starts = jnp.sum(below, axis=1) + turns * row_slots.shape[0]
    return jnp.concatenate([starts, (own_index % GROUP)[None]])


def pattern_table(starts, row_slots, columns, slot_count):
    rows = row_slots.shape[0]
    span = GROUP * slot_count + 2 * REACH
    row = starts[SHIFTS] - REACH + jnp.arange(span, dtype=jnp.int32)
    row = jnp.where(row < 0, row + rows, row)
    row = jnp.where(row >= rows, row - rows, row)
    found = jnp.take(columns, jnp.take(row_slots, row), axis=0) - row[:, None]
    found = jnp.where(found > rows // 2, found - rows, found)
    found = jnp.where(found < -(rows // 2), found + rows, found)
    wanted = jnp.arange(-BAND, BAND + 1, dtype=jnp.int32)
    order = jnp.arange(1, columns.shape[1] + 1, dtype=jnp.int32)
    which = jnp.sum(jnp.where(found[:, None, :] == wanted[None, :, None], order, 0), axis=2) - 1
    return jnp.concatenate([starts, jnp.clip(found, -BAND, BAND).reshape(-1), which.reshape(-1)])


class Rows:
    def __init__(self, table, row_tiles, slot_count):
        self.table = table
        self.row_tiles = row_tiles
        self.slot_count = slot_count
        self.core = table[STARTS - 1]
        self.middle = table[STARTS - 2]
        self.offsets = STARTS
        self.which = STARTS + (GROUP * slot_count + 2 * REACH) * row_tiles

    def group(self, step):
        return self.table[SHIFTS + step]

    def edge(self, shift, forward):
        return jnp.where(forward, self.group(shift), self.group(1 - shift))

    def place(self, row):
        return jnp.clip(row - self.group(0) + REACH, 0, GROUP * self.slot_count + 2 * REACH - 1)

    def offset(self, row, t):
        return self.table[self.offsets + self.place(row) * self.row_tiles + t]

    def tile_at(self, row, offset):
        return self.table[self.which + self.place(row) * (2 * BAND + 1) + offset + BAND]

    def group_tile(self, row):
        low = self.group(0)
        middle = self.middle
        slot = jnp.where(row < middle, row - low, row - middle + self.slot_count)
        return jnp.clip(slot, 0, GROUP * self.slot_count - 1) * self.row_tiles


def split(value):
    high = value.astype(jnp.bfloat16)
    return high, (value - high.astype(jnp.float32)).astype(jnp.bfloat16)


def eye(tile):
    return lax.broadcasted_iota(jnp.int32, (tile, tile), 0) == lax.broadcasted_iota(
        jnp.int32, (tile, tile), 1
    )


def inverse_column(block):
    tile = block.shape[-1]
    return 1.0 / jnp.sum(jnp.where(eye(tile), block, 0.0), axis=1, keepdims=True)


def inverse_row(block):
    tile = block.shape[-1]
    return 1.0 / jnp.sum(jnp.where(eye(tile), block, 0.0), axis=0, keepdims=True)


def near_pack_kernel(row_tiles, slot_count, starts, own, other, near, next_near, sems):
    rows = Rows(starts, row_tiles, slot_count)
    forward = rows.core == 0
    held = slot_count * row_tiles
    wanted = []
    for shift, ref, distances in ((1, near, range(2, BAND + 1)), (2, next_near, (BAND,))):
        for i, d in enumerate(distances):
            edge = rows.edge(shift, forward)
            base = rows.group_tile(jnp.where(forward, edge - d, edge + d - 1))
            wanted.append((base, ref.at[pl.ds(i * row_tiles, row_tiles)]))
    for i, (base, place) in enumerate(wanted):
        second = base >= held
        mine = jnp.where(second, 1, 0) == rows.core
        start = jnp.where(second, base - held, base)

        @pl.when(mine)
        def take_own():
            pltpu.make_async_copy(own.at[pl.ds(start, row_tiles)], place, sems.at[i]).start()

        @pl.when(jnp.logical_not(mine))
        def take_other():
            pltpu.make_async_copy(other.at[pl.ds(start, row_tiles)], place, sems.at[i]).start()

    for i, (base, place) in enumerate(wanted):
        pltpu.make_async_copy(own.at[pl.ds(0, row_tiles)], place, sems.at[i]).wait()


def far_pack_kernel(row_tiles, slot_count, starts, own, other, *rest):
    outs = rest[:SHIFTS]
    pool, sems = rest[SHIFTS:]
    core = starts[STARTS - 1]
    rows = Rows(starts, row_tiles, slot_count)
    held = slot_count * row_tiles
    own_copy = pltpu.make_async_copy(own, pool.at[pl.ds(core * held, held)], sems.at[0])
    other_copy = pltpu.make_async_copy(other, pool.at[pl.ds((1 - core) * held, held)], sems.at[1])
    own_copy.start()
    other_copy.start()
    own_copy.wait()
    other_copy.wait()
    forward = core == 0
    sign = jnp.where(forward, 1, -1)
    for shift in range(1, SHIFTS + 1):
        edge = rows.edge(shift, forward)
        slots = far_slots(shift)
        for d in sorted({d for d, _ in slots}):
            row = jnp.where(forward, edge - d, edge + d - 1)
            base = rows.group_tile(row)
            scale = -inverse_column(pool[base])
            for at, (distance, step) in enumerate(slots):
                if distance == d:
                    t = rows.tile_at(row, sign * step)
                    factor = jnp.where(t > 0, scale, 0.0)
                    outs[shift - 1][at] = factor * pool[base + jnp.maximum(t, 0)]


def dot(a, b):
    return jnp.dot(a, b, preferred_element_type=jnp.float32)


def near_kernel(row_tiles, slot_count, starts, own, other, edge, near_rows, next_rows,
                edge_p, near_p, next_p, out, a_high, a_low, b_high, b_low, inv_out,
                pool, left_high, left_low, y_high, y_low, p_high, p_low,
                inv_row, offsets, y_at, p_at, whole, sems):
    core = starts[2 * SHIFTS + 3]
    rows = Rows(starts, row_tiles, slot_count)
    tile = own.shape[-1]
    width = 2 * BAND + 1
    first = jnp.where(core == 0, rows.group(0), rows.middle)
    count = jnp.where(core == 0, rows.middle, rows.group(1)) - first
    near = count + 2 * BAND
    low = rows.group(0)
    high = rows.group(1)
    near_behind = low - rows.group(-1)
    near_ahead = rows.group(2) - high
    zero_y = y_high.shape[0] - 1
    zero_p = p_high.shape[0] - 1
    nothing = jnp.zeros((tile, tile), jnp.bfloat16)
    y_high[zero_y] = nothing
    y_low[zero_y] = nothing
    p_high[zero_p] = nothing
    p_low[zero_p] = nothing

    def fetch(w, carry):
        row = first - REACH + w
        behind = row < low
        ahead = row >= high
        outside = behind | ahead
        inside = jnp.logical_not(outside)
        d = jnp.where(behind, low - row, row - high + 1)
        reached = jnp.where(behind, near_behind, near_ahead)
        mine = outside & (jnp.where(behind, 0, 1) == core)
        theirs = outside & (jnp.where(behind, 0, 1) != core)
        home = inside & (jnp.where(row < rows.middle, 0, 1) == core)
        slot = jnp.where(row < rows.middle, row - low, row - rows.middle)
        whole[w] = jnp.where(inside | (d <= BAND), 1, 0)
        choices = [(home, own, slot), (inside & jnp.logical_not(home), other, slot)]
        for side, refs in ((mine, (edge, near_rows, next_rows)), (theirs, (edge_p, near_p, next_p))):
            choices.append((side & (d == 1), refs[0], 0))
            choices.append((side & (d > 1) & (d <= BAND) & (d <= reached), refs[1], d - 2))
            choices.append((side & (d == BAND) & (d > reached), refs[2], 0))
        for chosen, ref, at in choices:

            @pl.when(chosen)
            def take():
                pltpu.make_async_copy(
                    ref.at[pl.ds(at * row_tiles, row_tiles)], pool.at[pl.ds(w * row_tiles, row_tiles)], sems.at[w]
                ).start()

        return carry

    lax.fori_loop(0, near + 2 * BAND, fetch, 0)

    def clear_y(i, carry):
        y_at[i] = zero_y
        return carry

    def clear_p(i, carry):
        p_at[i] = zero_p
        return carry

    lax.fori_loop(0, y_at.shape[0], clear_y, 0, unroll=8)
    lax.fori_loop(0, p_at.shape[0], clear_p, 0, unroll=7)

    def arrive(w, carry):
        @pl.when(whole[w] == 1)
        def wait():
            place = pool.at[pl.ds(w * row_tiles, row_tiles)]
            pltpu.make_async_copy(own.at[pl.ds(0, row_tiles)], place, sems.at[w]).wait()

        return carry

    lax.fori_loop(0, near + 2 * BAND, arrive, 0)

    def invert(f, carry):
        inv_row[f] = inverse_row(pool[(f + BAND) * row_tiles])
        return carry

    lax.fori_loop(0, near, invert, 0)

    def near_row(f, carry):
        row = first - BAND + f
        base = (f + BAND) * row_tiles
        column = inverse_column(pool[base])
        for t in range(row_tiles):
            offset = rows.offset(row, t)
            offsets[f * row_tiles + t] = offset
            block = pool[base + t]
            high_part, low_part = split(block)
            left_high[f, :, pl.ds(t * tile, tile)] = high_part
            left_low[f, :, pl.ds(t * tile, tile)] = low_part
            c = f + offset
            inside = (c >= 0) & (c < near)
            value = -(column * block) * inv_row[jnp.clip(c, 0, near - 1)]
            if t == 0:
                value = value + jnp.where(eye(tile), 2.0 * column, 0.0)
            high_part, low_part = split(value)
            at = (f + BAND) * width + offset + BAND
            y_high[at] = high_part
            y_low[at] = low_part
            y_at[at] = jnp.where(inside, at, zero_y)
            p_at[f * width + offset + BAND] = f * row_tiles + t
        return carry

    lax.fori_loop(0, near, near_row, 0)

    def far_row(e, carry):
        behind = e < BAND
        sign = jnp.where(behind, 1, -1)
        d = jnp.where(behind, REACH - e, e + 1)
        w = jnp.where(behind, e, near + e)
        row = first - REACH + w

        @pl.when(whole[w] == 1)
        def build():
            scale = -inverse_column(pool[w * row_tiles])
            for step in range(1, BAND + 1):
                offset = sign * step
                t = rows.tile_at(row, offset)
                at = w * width + offset + BAND

                @pl.when((t > 0) & (step >= d - BAND))
                def keep():
                    c = jnp.clip(w - BAND + offset, 0, near - 1)
                    high_part, low_part = split((scale * pool[w * row_tiles + t]) * inv_row[c])
                    y_high[at] = high_part
                    y_low[at] = low_part
                    y_at[at] = at

        return carry

    lax.fori_loop(0, 2 * BAND, far_row, 0)

    def gathered(table, start, zero, high_ref, low_ref, f, lefts):
        steps = [offsets[f * row_tiles + t] for t in range(row_tiles)]
        at = []
        for t in range(row_tiles):
            line = []
            for v in range(row_tiles):
                ahead = steps[v] - steps[t]
                inside = (ahead >= -BAND) & (ahead <= BAND)
                place = (start + steps[t]) * width + jnp.clip(ahead, -BAND, BAND) + BAND
                line.append(jnp.where(inside, table[place], zero))
            at.append(line)
        left_h, left_l = lefts
        results = []
        for v in range(0, row_tiles, 2):
            pair = range(v, min(v + 2, row_tiles))

            def right(ref):
                lines = [jnp.concatenate([ref[at[t][c]] for c in pair], axis=1) for t in range(row_tiles)]
                return jnp.concatenate(lines, axis=0)

            high_right = right(high_ref)
            value = dot(left_h, high_right) + dot(left_l, high_right) + dot(left_h, right(low_ref))
            for i in range(len(pair)):
                results.append(value[:, i * tile : (i + 1) * tile])
        return results

    def product_row(f, carry):
        values = gathered(y_at, f + BAND, zero_y, y_high, y_low, f, (left_high[f], left_low[f]))
        for t, value in enumerate(values):
            high_part, low_part = split(value)
            p_high[f * row_tiles + t] = high_part
            p_low[f * row_tiles + t] = low_part
        return carry

    lax.fori_loop(0, near, product_row, 0)

    def own_row(j, carry):
        f = j + BAND
        tiles = []
        for t in range(row_tiles):
            at = (f + BAND) * width + offsets[f * row_tiles + t] + BAND
            tiles.append((y_high[at], y_low[at]))
        lefts = [jnp.concatenate([pair[i] for pair in tiles], axis=1) for i in range(2)]
        values = gathered(p_at, f, zero_p, p_high, p_low, f, lefts)
        for t, value in enumerate(values):
            high_part, low_part = tiles[t]
            out[j * row_tiles + t] = 2.0 * (high_part.astype(jnp.float32) + low_part.astype(jnp.float32)) - value
        return carry

    lax.fori_loop(0, count, own_row, 0)

    def empty_row(j, carry):
        for t in range(row_tiles):
            out[j * row_tiles + t] = jnp.zeros((tile, tile), jnp.float32)
        return carry

    lax.fori_loop(count, slot_count, empty_row, 0)

    a_high[...] = jnp.zeros_like(a_high)
    a_low[...] = jnp.zeros_like(a_low)
    b_high[...] = jnp.zeros_like(b_high)
    b_low[...] = jnp.zeros_like(b_low)
    for side in range(2):
        sign = -1 if side == 0 else 1
        for e in range(1, BAND + 1):
            f = BAND - e if side == 0 else near - BAND + e - 1
            row = first - BAND + f
            inv_out[side * BAND + e - 1] = inv_row[f]
            for d in range(BAND + 1, REACH + 1):
                if d - e <= BAND:
                    t = rows.tile_at(row, sign * (d - e))
                    here = (side, pl.ds((e - 1) * tile, tile), pl.ds((d - BAND - 1) * tile, tile))

                    @pl.when(t > 0)
                    def keep_a():
                        lanes = pl.ds(pl.multiple_of(t * tile, tile), tile)
                        a_high[here] = left_high[f, :, lanes]
                        a_low[here] = left_low[f, :, lanes]

            for i in range(BAND + 1 - e):
                w = REACH + i if side == 0 else REACH + count - 1 - i
                at = y_at[w * width + sign * (i + e) + BAND]
                here = (side, pl.ds(i * tile, tile), pl.ds((e - 1) * tile, tile))

                @pl.when(i < count)
                def keep_b():
                    b_high[here] = y_high[at]
                    b_low[here] = y_low[at]


def far_kernel(row_tiles, slot_count, starts, estimate, a_high_in, a_low_in, b_high_in, b_low_in, inv_in, *rest):
    arrays = rest[: 2 * SHIFTS]
    out, a_high, a_low, b_high, b_low, inv_rows, far, changed, y_high, y_low, sems, row_sems = rest[2 * SHIFTS :]
    core = starts[STARTS - 1]
    rows = Rows(starts, row_tiles, slot_count)
    tile = changed.shape[-1]
    first = jnp.where(core == 0, rows.group(0), rows.middle)
    count = jnp.where(core == 0, rows.middle, rows.group(1)) - first
    pairs = [(a_high_in, a_high), (a_low_in, a_low), (b_high_in, b_high), (b_low_in, b_low), (inv_in, inv_rows)]
    base = 0
    bases = []
    for array in arrays:
        bases.append(base)
        pairs.append((array, far.at[pl.ds(base, array.shape[0])]))
        base += array.shape[0]
    copies = [pltpu.make_async_copy(*pair, sems.at[i]) for i, pair in enumerate(pairs)]
    for copy in reversed(copies):
        copy.start()
    targets = []
    for side in range(2):
        sign = -1 if side == 0 else 1
        for i in range(BAND):
            for e in range(1, BAND + 1 - i):
                j = i if side == 0 else count - 1 - i
                t = rows.tile_at(first + j, sign * (i + e))
                targets.append((side, i, e, (i < count) & (t > 0), j * row_tiles + t))
    for at, (side, i, e, present, place) in enumerate(targets):

        @pl.when(present)
        def read():
            pltpu.make_async_copy(estimate.at[place], changed.at[at], row_sems.at[at]).start()

    y_high[...] = jnp.zeros_like(y_high)
    y_low[...] = jnp.zeros_like(y_low)
    for copy in copies[4:]:
        copy.wait()
    for side in range(2):
        direct = core == side
        between = jnp.where(direct, 0, first - rows.group(0) if side == 0 else rows.group(1) - first - count)
        one = rows.group(0) - rows.group(-1) if side == 0 else rows.group(2) - rows.group(1)
        two = rows.group(0) - rows.group(-2) if side == 0 else rows.group(3) - rows.group(1)
        for d, step in FAR:
            e = d - step
            here = (side, pl.ds((d - BAND - 1) * tile, tile), pl.ds((e - 1) * tile, tile))
            beyond = d - between
            place = jnp.int32(0)
            for distance, other_step in FAR:
                if other_step == step and distance <= d:
                    for shift in reversed(range(1, SHIFTS + 1)):
                        slots = far_slots(shift)
                        if (distance, step) in slots:
                            at = slots.index((distance, step))
                            at = jnp.where(direct, bases[shift - 1] + at, bases[SHIFTS + shift - 1] + at)
                            held = jnp.bool_(True) if shift == SHIFTS else beyond <= (one, two)[shift - 1]
                            place = jnp.where((beyond == distance) & held, at, place)
            value = jnp.where(beyond > BAND, far[place] * inv_rows[side * BAND + e - 1], 0.0)
            high_part, low_part = split(value)
            y_high[here] = high_part
            y_low[here] = low_part
    for copy in copies[:4]:
        copy.wait()
    for side in range(2):
        sign = -1 if side == 0 else 1
        extra = dot(a_high[side], y_high[side]) + dot(a_high[side], y_low[side])
        extra = extra + dot(a_low[side], y_high[side])
        bands = []
        for k in range(1, BAND + 1):
            parts = []
            for e in range(1, BAND + 1):
                part = extra[(k - 1) * tile : k * tile, (e - 1) * tile : e * tile]
                if k != e:
                    row = first - k if side == 0 else first + count + k - 1
                    part = jnp.where(rows.tile_at(row, sign * (e - k)) > 0, part, 0.0)
                parts.append(part)
            bands.append(jnp.concatenate(parts, axis=1))
        extra_high, extra_low = split(jnp.concatenate(bands, axis=0))
        change = dot(b_high[side], extra_high) + dot(b_high[side], extra_low)
        change = change + dot(b_low[side], extra_high)
        for at, (of, i, e, present, place) in enumerate(targets):
            if of == side:
                part = change[i * tile : (i + 1) * tile, (e - 1) * tile : e * tile]

                @pl.when(present)
                def update():
                    pltpu.make_async_copy(estimate.at[place], changed.at[at], row_sems.at[at]).wait()
                    changed[at] -= part
                    pltpu.make_async_copy(changed.at[at], out.at[place], row_sems.at[at]).start()

    for at, (side, i, e, present, place) in enumerate(targets):

        @pl.when(present)
        def finish():
            pltpu.make_async_copy(changed.at[at], out.at[place], row_sems.at[at]).wait()


def estimate_rows(coupling, columns, row_slots):
    slot_count, row_tiles, tile, _ = coupling.shape
    devices = lax.axis_size("rows")
    own_index = lax.axis_index("rows")
    held = slot_count * row_tiles
    near = slot_count + 2 * BAND
    width = 2 * BAND + 1
    reach = BAND * tile
    own = coupling.reshape(held, tile, tile)
    listed = range(devices)
    smem = pl.BlockSpec(memory_space=pltpu.SMEM)
    hbm = pl.BlockSpec(memory_space=pltpu.HBM)
    vmem = pl.BlockSpec(memory_space=pltpu.VMEM)

    def blocks(count, dtype=jnp.float32):
        return jax.ShapeDtypeStruct((count, tile, tile), dtype)

    def partner(value):
        return lax.ppermute(value, "rows", [(i, i ^ 1) for i in listed])

    def along(value, step):
        return lax.ppermute(value, "rows", [(i, (i + (-step if i % GROUP else step)) % devices) for i in listed])

    other = partner(own)
    starts = group_starts(row_slots, slot_count, devices, own_index)
    last = starts[SHIFTS + 1] - 1 - starts[2 * SHIFTS + 2]
    edge_row = jnp.where(own_index % GROUP == 0, 0, last) * row_tiles
    edge_out = lax.dynamic_slice_in_dim(own, edge_row, row_tiles, 0)
    edge = along(edge_out, -1)
    near_out, next_out = pl.pallas_call(
        lambda *refs: near_pack_kernel(row_tiles, slot_count, *refs),
        out_shape=[blocks((BAND - 1) * row_tiles), blocks(row_tiles)],
        in_specs=[smem] + [hbm] * 2,
        out_specs=[vmem] * 2,
        scratch_shapes=[pltpu.SemaphoreType.DMA((BAND,))],
        name="near_pack",
    )(starts, own, other)
    near_rows = along(near_out, GROUP)
    next_rows = along(next_out, 2 * GROUP)
    table = pattern_table(lax.optimization_barrier((starts, near_out))[0], row_slots, columns, slot_count)
    far_out = pl.pallas_call(
        lambda *refs: far_pack_kernel(row_tiles, slot_count, *refs),
        out_shape=[blocks(len(far_slots(shift))) for shift in range(1, SHIFTS + 1)],
        in_specs=[smem] + [hbm] * 2,
        out_specs=[vmem] * SHIFTS,
        scratch_shapes=[
            pltpu.VMEM((GROUP * held, tile, tile), jnp.float32),
            pltpu.SemaphoreType.DMA((2,)),
        ],
        name="far_pack",
    )(table, own, other)
    passed = []
    for value in (edge, near_rows, next_rows):
        passed.append(partner(value))
    far_out = lax.optimization_barrier((tuple(far_out), near_rows))[0]
    far_in = []
    for shift in range(1, SHIFTS + 1):
        far_in.append(along(far_out[shift - 1], GROUP * shift))
    rows_of = near * row_tiles
    table_size = (near + 2 * BAND) * width
    side_block = jax.ShapeDtypeStruct((2, reach, reach), jnp.bfloat16)
    estimate, *shares = pl.pallas_call(
        lambda *refs: near_kernel(row_tiles, slot_count, *refs),
        out_shape=[blocks(held)] + [side_block] * 4 + [jax.ShapeDtypeStruct((2 * BAND, 1, tile), jnp.float32)],
        in_specs=[smem] + [hbm] * 8,
        out_specs=[vmem] * 6,
        scratch_shapes=[
            pltpu.VMEM(((near + 2 * BAND) * row_tiles, tile, tile), jnp.float32),
            pltpu.VMEM((near, tile, row_tiles * tile), jnp.bfloat16),
            pltpu.VMEM((near, tile, row_tiles * tile), jnp.bfloat16),
            pltpu.VMEM((table_size + 1, tile, tile), jnp.bfloat16),
            pltpu.VMEM((table_size + 1, tile, tile), jnp.bfloat16),
            pltpu.VMEM((rows_of + 1, tile, tile), jnp.bfloat16),
            pltpu.VMEM((rows_of + 1, tile, tile), jnp.bfloat16),
            pltpu.VMEM((near, 1, tile), jnp.float32),
            pltpu.SMEM((rows_of,), jnp.int32),
            pltpu.SMEM((table_size,), jnp.int32),
            pltpu.SMEM((near * width,), jnp.int32),
            pltpu.SMEM((near + 2 * BAND,), jnp.int32),
            pltpu.SemaphoreType.DMA((near + 2 * BAND,)),
        ],
        cost_estimate=pl.CostEstimate(flops=4 * 10**9, bytes_accessed=10**7, transcendentals=0),
        name="near_rows",
    )(table, own, other, edge, near_rows, next_rows, *passed)
    far_passed = []
    for shift in range(1, SHIFTS + 1):
        far_passed.append(partner(far_in[shift - 1]))
    targets = BAND * (BAND + 1)
    out = pl.pallas_call(
        lambda *refs: far_kernel(row_tiles, slot_count, *refs),
        out_shape=blocks(held),
        in_specs=[smem] + [hbm] * (6 + 2 * SHIFTS),
        out_specs=hbm,
        scratch_shapes=[pltpu.VMEM((2, reach, reach), jnp.bfloat16)] * 4
        + [
            pltpu.VMEM((2 * BAND, 1, tile), jnp.float32),
            pltpu.VMEM((2 * sum(len(far_slots(shift)) for shift in range(1, SHIFTS + 1)), tile, tile), jnp.float32),
            pltpu.VMEM((targets, tile, tile), jnp.float32),
            pltpu.VMEM((2, reach, reach), jnp.bfloat16),
            pltpu.VMEM((2, reach, reach), jnp.bfloat16),
            pltpu.SemaphoreType.DMA((5 + 2 * SHIFTS,)),
            pltpu.SemaphoreType.DMA((targets,)),
        ],
        input_output_aliases={1: 0},
        name="far_rows",
    )(table, estimate, *shares, *far_in, *far_passed)
    return out.reshape(coupling.shape)


def solution(mesh):
    return jax.shard_map(
        estimate_rows,
        mesh=mesh,
        in_specs=(P("rows", None, None, None), P(), P()),
        out_specs=P("rows", None, None, None),
        check_vma=False,
    )
```

time: 281 us -> 92.6 us (0.33)
  the two profiles are of different devices: /device:TPU:0 before, /device:TPU:1 now
where the time goes in v1:
time: 92.6 us; the launch traced here: 92.2 us
  Pallas kernels  29.9 us (32%)
  waiting for transfers between devices  25.3 us (27%)
  starting transfers between devices  24.6 us (27%)
  local copies, waits for them, and re-layouts  7.57 us (8%)
  other arithmetic  2.56 us (3%)
  between operations  2.22 us (2%)
    ppermute x6, waiting for transfers between devices, along(): lax.ppermute(value, 'rows', [(i, (i + (-step if i % GROUP else step)) % d...  25.3 us
    pallas_call x1, Pallas kernels, estimate_rows(): pl.pallas_call(lambda *refs: near_kernel(row_tiles, slot_count, *refs), o...  16.4 us
    ppermute x6, starting transfers between devices, along(): lax.ppermute(value, 'rows', [(i, (i + (-step if i % GROUP else step)) % d...  14.9 us
    ppermute x7, starting transfers between devices, partner(): return lax.ppermute(value, 'rows', [(i, i ^ 1) for i in listed])  9.78 us
    pallas_call x1, Pallas kernels, estimate_rows(): pl.pallas_call(lambda *refs: far_kernel(row_tiles, slot_count, *refs), ou...  7.14 us
    unnamed x23, local copies, waits for them, and re-layouts  3.62 us
    pallas_call x1, Pallas kernels, estimate_rows(): pl.pallas_call(lambda *refs: far_pack_kernel(row_tiles, slot_count, *refs...  3.51 us
    pallas_call x1, Pallas kernels, estimate_rows(): pl.pallas_call(lambda *refs: near_pack_kernel(row_tiles, slot_count, *ref...  2.83 us
  transfers between devices with their start and end apart: 13, of which 4 were waited for; matrix products, arithmetic and copies ran while one was open for 8% of the time, Pallas kernels for 25%

profile of v1, /device:TPU:1, one launch (start us, length us, event | category | flops | bytes accessed | tf_op | source)
XLA Modules:
  0.0 92.2 jit_solution(9135197667723165788)
XLA Ops:
  0.0 0.0 collective-permute-start
  0.0 0.1 add_multiply_fusion
  0.1 0.8 convert_reduce_fusion
  0.9 0.1 fusion.2
  1.0 0.7 fusion.4
  3.0 1.0 %constant_dynamic-slice_fusion = f32[5,128,128]{2,1,0:T(8,128)S(1)} fusion(f32[20,128,128]{2,1,0:T(8,128)} %bitcast.15, s32[]{:T(128)S(6)} %select_n.180), kind=kLoop, calls=%fused_computation.39 | loop fusion | bytes 655364 | tf_op jit(solution)/shard_map/dynamic_slice | solution.py:507
  4.0 2.6 %collective-permute-start.1 = (f32[5,128,128]{2,1,0:T(8,128)S(1)}, f32[5,128,128]{2,1,0:T(8,128)}, u32[]{:S(2)}, u32[]{:S(2)}) collective-permute-start(f32[5,128,128]{2,1,0:T(8,128)S(1)} %constant_dynamic-slice_fusion), channel_id=1, source_target_pairs={{0,31},{1,2},{2,1},{3,4},{4,3},{5,6},{6,5},{7,8},{8,7},{9,10},{10,... | collective-permute-start | bytes 983048 | tf_op jit(solution)/shard_map/ppermute | solution.py:501
  6.7 0.8 copy.7
  7.5 0.7 pad_add_fusion.1.refs_0_
  8.1 0.0 copy-start.8
  8.1 0.0 copy-start
  8.1 6.3 %collective-permute-done.1.refs_3_ = f32[5,128,128]{2,1,0:T(8,128)} collective-permute-done((f32[5,128,128]{2,1,0:T(8,128)S(1)}, f32[5,128,128]{2,1,0:T(8,128)}, u32[]{:S(2)}, u32[]{:S(2)}) %collective-permute-start.1) | collective-permute-done | bytes 327712 | tf_op jit(solution)/shard_map/ppermute | solution.py:501
  14.4 1.7 %collective-permute-start.4 = (f32[5,128,128]{2,1,0:T(8,128)}, f32[5,128,128]{2,1,0:T(8,128)}, u32[]{:S(2)}, u32[]{:S(2)}) collective-permute-start(f32[5,128,128]{2,1,0:T(8,128)} %collective-permute-done.1.refs_3_), channel_id=1, source_target_pairs={{0,1},{1,0},{2,3},{3,2},{4,5},{5,4},{6,7},{7,6},{8,9},{9,8},{10,11... | collective-permute-start | bytes 983048 | tf_op jit(solution)/shard_map/ppermute | solution.py:498
  16.1 0.0 collective-permute-done.refs_2_
  16.1 1.1 %copy-done.1 = f32[20,128,128]{2,1,0:T(8,128)} copy-done((f32[20,128,128]{2,1,0:T(8,128)}, f32[20,128,128]{2,1,0:T(8,128)S(1)}, u32[]{:S(2)}) %copy-start.1) | copy-done | bytes 1310744
  17.2 2.8 %near_pack.1 = (f32[10,128,128]{2,1,0:T(8,128)}, f32[5,128,128]{2,1,0:T(8,128)}) custom-call(s32[10]{0:T(128)} %pad_add_fusion.1.refs_0_, f32[20,128,128]{2,1,0:T(8,128)} %bitcast.16, f32[20,128,128]{2,1,0:T(8,128)} %copy-done.1), custom_call_target="tpu_custom_call" | custom-call | tf_op jit(solution)/shard_map/near_pack/pallas_call | solution.py:509
  20.0 0.0 copy-done.8
  20.1 0.6 slice.9
  21.4 0.0 copy-done
  21.4 0.7 gather_fusion
  22.2 4.9 %collective-permute-start.2 = (f32[10,128,128]{2,1,0:T(8,128)}, f32[10,128,128]{2,1,0:T(8,128)S(1)}, u32[]{:S(2)}, u32[]{:S(2)}) collective-permute-start(f32[10,128,128]{2,1,0:T(8,128)} %get-tuple-element.20), channel_id=1, source_target_pairs={{0,2},{1,31},{2,4},{3,1},{4,6},{5,3},{6,8},{7,5},{8,10},{9,7},{10,... | collective-permute-start | bytes 1966088 | tf_op jit(solution)/shard_map/ppermute | solution.py:501
  27.1 0.6 gather_fusion.1
  27.6 0.1 compare_select_fusion
  27.7 0.1 copy.8
  27.8 0.1 sub.68
  27.9 0.5 collective-permute-start.3
  28.4 0.1 select_reduce_fusion
  28.5 9.2 %collective-permute-done.2.refs_4_ = f32[10,128,128]{2,1,0:T(8,128)S(1)} collective-permute-done((f32[10,128,128]{2,1,0:T(8,128)}, f32[10,128,128]{2,1,0:T(8,128)S(1)}, u32[]{:S(2)}, u32[]{:S(2)}) %collective-permute-start.2) | collective-permute-done | bytes 655392 | tf_op jit(solution)/shard_map/ppermute | solution.py:501
  37.6 2.7 %collective-permute-start.5 = (f32[10,128,128]{2,1,0:T(8,128)S(1)}, f32[10,128,128]{2,1,0:T(8,128)S(1)}, u32[]{:S(2)}, u32[]{:S(2)}) collective-permute-start(f32[10,128,128]{2,1,0:T(8,128)S(1)} %collective-permute-done.2.refs_4_), channel_id=1, source_target_pairs={{0,1},{1,0},{2,3},{3,2},{4,5},{5,4},{6,7},{7,6},{8,9},{9,8},{10,11... | collective-permute-start | bytes 1966088 | tf_op jit(solution)/shard_map/ppermute | solution.py:498
  40.3 0.1 copy.9
  40.4 0.1 sub.72
  40.5 0.7 pad_add_fusion.refs_0_
  41.2 3.5 %far_pack.1 = (f32[6,128,128]{2,1,0:T(8,128)}, f32[6,128,128]{2,1,0:T(8,128)}, f32[3,128,128]{2,1,0:T(8,128)}) custom-call(s32[250]{0:T(256)} %pad_add_fusion.refs_0_, f32[20,128,128]{2,1,0:T(8,128)} %bitcast.17, f32[20,128,128]{2,1,0:T(8,128)} %copy-done.1), custom_call_target="tpu_custom_call" | custom-call | tf_op jit(solution)/shard_map/far_pack/pallas_call | solution.py:520
  44.7 0.0 copy-done.9
  44.7 4.3 %collective-permute-start.7 = (f32[6,128,128]{2,1,0:T(8,128)}, f32[6,128,128]{2,1,0:T(8,128)S(1)}, u32[]{:S(2)}, u32[]{:S(2)}) collective-permute-start(f32[6,128,128]{2,1,0:T(8,128)} %get-tuple-element.32), channel_id=1, source_target_pairs={{0,2},{1,31},{2,4},{3,1},{4,6},{5,3},{6,8},{7,5},{8,10},{9,7},{10,... | collective-permute-start | bytes 1179656 | tf_op jit(solution)/shard_map/ppermute | solution.py:501
  49.0 1.2 %collective-permute-start.8 = (f32[6,128,128]{2,1,0:T(8,128)}, f32[6,128,128]{2,1,0:T(8,128)S(1)}, u32[]{:S(2)}, u32[]{:S(2)}) collective-permute-start(f32[6,128,128]{2,1,0:T(8,128)} %get-tuple-element.33), channel_id=1, source_target_pairs={{0,4},{1,29},{2,6},{3,31},{4,8},{5,1},{6,10},{7,3},{8,12},{9,5},{1... | collective-permute-start | bytes 1179656 | tf_op jit(solution)/shard_map/ppermute | solution.py:501
  50.2 0.0 collective-permute-done.3.refs_5_
  50.3 0.0 collective-permute-start.6
  50.3 0.0 collective-permute-done.4.refs_6_
  50.3 1.3 %collective-permute-start.9 = (f32[3,128,128]{2,1,0:T(8,128)}, f32[3,128,128]{2,1,0:T(8,128)S(1)}, u32[]{:S(2)}, u32[]{:S(2)}) collective-permute-start(f32[3,128,128]{2,1,0:T(8,128)} %get-tuple-element.34), channel_id=1, source_target_pairs={{0,6},{1,27},{2,8},{3,29},{4,10},{5,31},{6,12},{7,1},{8,14},{9,3},... | collective-permute-start | bytes 589832 | tf_op jit(solution)/shard_map/ppermute | solution.py:501
  51.6 2.7 %collective-permute-done.7.refs_7_ = f32[6,128,128]{2,1,0:T(8,128)S(1)} collective-permute-done((f32[6,128,128]{2,1,0:T(8,128)}, f32[6,128,128]{2,1,0:T(8,128)S(1)}, u32[]{:S(2)}, u32[]{:S(2)}) %collective-permute-start.7) | collective-permute-done | bytes 393248 | tf_op jit(solution)/shard_map/ppermute | solution.py:501
  54.3 4.9 %collective-permute-start.10 = (f32[6,128,128]{2,1,0:T(8,128)S(1)}, f32[6,128,128]{2,1,0:T(8,128)S(1)}, u32[]{:S(2)}, u32[]{:S(2)}) collective-permute-start(f32[6,128,128]{2,1,0:T(8,128)S(1)} %collective-permute-done.7.refs_7_), channel_id=1, source_target_pairs={{0,1},{1,0},{2,3},{3,2},{4,5},{5,4},{6,7},{7,6},{8,9},{9,8},{10,11... | collective-permute-start | bytes 1179656 | tf_op jit(solution)/shard_map/ppermute | solution.py:498
  59.2 7.1 %collective-permute-done.8.refs_8_ = f32[6,128,128]{2,1,0:T(8,128)S(1)} collective-permute-done((f32[6,128,128]{2,1,0:T(8,128)}, f32[6,128,128]{2,1,0:T(8,128)S(1)}, u32[]{:S(2)}, u32[]{:S(2)}) %collective-permute-start.8) | collective-permute-done | bytes 393248 | tf_op jit(solution)/shard_map/ppermute | solution.py:501
  66.3 0.0 collective-permute-start.11
  66.3 0.0 collective-permute-done.9.refs_9_
  66.3 0.0 copy-start.6
  66.3 0.5 collective-permute-start.12
  66.8 0.0 collective-permute-done.6.refs_8_
  66.8 0.0 collective-permute-done.5.refs_7_
  66.8 0.8 copy-done.10
  67.7 16.4 %near_rows.1 = (f32[20,128,128]{2,1,0:T(8,128)}, bf16[2,384,384]{2,1,0:T(8,128)(2,1)}, bf16[2,384,384]{2,1,0:T(8,128)(2,1)}, bf16[2,384,384]{2,1,0:T(8,128)(2,1)...) custom-call(s32[250]{0:T(256)} %pad_add_fusion.refs_0_, f32[20,128,128]{2,1,0:T(8,128)} %bitcast.18, ...), custom_call_target="tpu_custom_call" | custom-call | flops 4000000000 | bytes 10000000 | tf_op jit(solution)/shard_map/near_rows/pallas_call | solution.py:541
  84.1 0.0 copy-done.2
  84.1 0.0 copy-done.3
  84.1 0.0 copy-done.6
  84.1 0.0 collective-permute-done.12.refs_12_
  84.1 0.0 copy-start.7
  84.2 0.0 collective-permute-done.10.refs_10_
  84.2 0.0 copy-start.4
  84.2 0.0 collective-permute-done.11.refs_11_
  84.2 0.0 copy-start.5
  84.2 0.6 copy-done.7
  84.8 0.1 copy-done.4
  85.0 0.1 copy-done.5
  85.1 7.1 %far_rows.1 = f32[20,128,128]{2,1,0:T(8,128)} custom-call(s32[250]{0:T(256)} %pad_add_fusion.refs_0_, f32[20,128,128]{2,1,0:T(8,128)} %get-tuple-element.23.refs_1_, bf16[2,384,384]{2,1,0:T(8,128)(2,1)} %get-tuple-element.24.refs_2_, bf16[2,384,384]{2,1,0:T(8,128)(2,1)} %get-tuple-element.25.refs_3_, ...), custom_call_target="tpu_custom_call", output_to_operand_aliasing={{}: (1, {})} | custom-call | tf_op jit(solution)/shard_map/far_rows/pallas_call | solution.py:568
  (16 shorter events, 0.1 us)
Async XLA Ops:
  0.0 16.1 %collective-permute-start = (f32[20,128,128]{2,1,0:T(8,128)}, f32[20,128,128]{2,1,0:T(8,128)S(1)}, u32[]{:S(2)}, u32[]{:S(2)}) collective-permute-start(f32[20,128,128]{2,1,0:T(8,128)} %bitcast.14), channel_id=1, source_target_pairs={{0,1},{1,0},{2,3},{3,2},{4,5},{5,4},{6,7},{7,6},{8,9},{9,8},{10,11... | collective-permute-start | bytes 3932168 | tf_op jit(solution)/shard_map/ppermute | solution.py:498
  4.0 10.4 %collective-permute-start.1 = (f32[5,128,128]{2,1,0:T(8,128)S(1)}, f32[5,128,128]{2,1,0:T(8,128)}, u32[]{:S(2)}, u32[]{:S(2)}) collective-permute-start(f32[5,128,128]{2,1,0:T(8,128)S(1)} %constant_dynamic-slice_fusion), channel_id=1, source_target_pairs={{0,31},{1,2},{2,1},{3,4},{4,3},{5,6},{6,5},{7,8},{8,7},{9,10},{10,... | collective-permute-start | bytes 983048 | tf_op jit(solution)/shard_map/ppermute | solution.py:501
  8.1 11.9 %copy-start.8 = (s32[10]{0:T(128)S(1)}, s32[10]{0:T(128)}, u32[]{:S(2)}) copy-start(s32[10]{0:T(128)} %pad_add_fusion.1.refs_0_) | copy-start | bytes 124
  8.1 13.3 %copy-start = (s32[64]{0:T(128)S(1)}, s32[64]{0:T(128)}, u32[]{:S(2)}) copy-start(s32[64]{0:T(128)} %param.5) | copy-start | bytes 772
  14.4 35.8 %collective-permute-start.4 = (f32[5,128,128]{2,1,0:T(8,128)}, f32[5,128,128]{2,1,0:T(8,128)}, u32[]{:S(2)}, u32[]{:S(2)}) collective-permute-start(f32[5,128,128]{2,1,0:T(8,128)} %collective-permute-done.1.refs_3_), channel_id=1, source_target_pairs={{0,1},{1,0},{2,3},{3,2},{4,5},{5,4},{6,7},{7,6},{8,9},{9,8},{10,11... | collective-permute-start | bytes 983048 | tf_op jit(solution)/shard_map/ppermute | solution.py:498
  16.1 1.1 %copy-start.1 = (f32[20,128,128]{2,1,0:T(8,128)}, f32[20,128,128]{2,1,0:T(8,128)S(1)}, u32[]{:S(2)}) copy-start(f32[20,128,128]{2,1,0:T(8,128)S(1)} %collective-permute-done.refs_2_) | copy-start | bytes 3932164
  22.2 15.5 %collective-permute-start.2 = (f32[10,128,128]{2,1,0:T(8,128)}, f32[10,128,128]{2,1,0:T(8,128)S(1)}, u32[]{:S(2)}, u32[]{:S(2)}) collective-permute-start(f32[10,128,128]{2,1,0:T(8,128)} %get-tuple-element.20), channel_id=1, source_target_pairs={{0,2},{1,31},{2,4},{3,1},{4,6},{5,3},{6,8},{7,5},{8,10},{9,7},{10,... | collective-permute-start | bytes 1966088 | tf_op jit(solution)/shard_map/ppermute | solution.py:501
  27.9 22.3 %collective-permute-start.3 = (f32[5,128,128]{2,1,0:T(8,128)}, f32[5,128,128]{2,1,0:T(8,128)}, u32[]{:S(2)}, u32[]{:S(2)}) collective-permute-start(f32[5,128,128]{2,1,0:T(8,128)} %get-tuple-element.22), channel_id=1, source_target_pairs={{0,4},{1,29},{2,6},{3,31},{4,8},{5,1},{6,10},{7,3},{8,12},{9,5},{1... | collective-permute-start | bytes 983048 | tf_op jit(solution)/shard_map/ppermute | solution.py:501
  37.6 7.1 %copy-start.9 = (f32[10,128,128]{2,1,0:T(8,128)}, f32[10,128,128]{2,1,0:T(8,128)S(1)}, u32[]{:S(2)}) copy-start(f32[10,128,128]{2,1,0:T(8,128)S(1)} %collective-permute-done.2.refs_4_) | copy-start | bytes 1966084
  37.6 29.2 %collective-permute-start.5 = (f32[10,128,128]{2,1,0:T(8,128)S(1)}, f32[10,128,128]{2,1,0:T(8,128)S(1)}, u32[]{:S(2)}, u32[]{:S(2)}) collective-permute-start(f32[10,128,128]{2,1,0:T(8,128)S(1)} %collective-permute-done.2.refs_4_), channel_id=1, source_target_pairs={{0,1},{1,0},{2,3},{3,2},{4,5},{5,4},{6,7},{7,6},{8,9},{9,8},{10,11... | collective-permute-start | bytes 1966088 | tf_op jit(solution)/shard_map/ppermute | solution.py:498
  44.7 9.6 %collective-permute-start.7 = (f32[6,128,128]{2,1,0:T(8,128)}, f32[6,128,128]{2,1,0:T(8,128)S(1)}, u32[]{:S(2)}, u32[]{:S(2)}) collective-permute-start(f32[6,128,128]{2,1,0:T(8,128)} %get-tuple-element.32), channel_id=1, source_target_pairs={{0,2},{1,31},{2,4},{3,1},{4,6},{5,3},{6,8},{7,5},{8,10},{9,7},{10,... | collective-permute-start | bytes 1179656 | tf_op jit(solution)/shard_map/ppermute | solution.py:501
  49.0 17.3 %collective-permute-start.8 = (f32[6,128,128]{2,1,0:T(8,128)}, f32[6,128,128]{2,1,0:T(8,128)S(1)}, u32[]{:S(2)}, u32[]{:S(2)}) collective-permute-start(f32[6,128,128]{2,1,0:T(8,128)} %get-tuple-element.33), channel_id=1, source_target_pairs={{0,4},{1,29},{2,6},{3,31},{4,8},{5,1},{6,10},{7,3},{8,12},{9,5},{1... | collective-permute-start | bytes 1179656 | tf_op jit(solution)/shard_map/ppermute | solution.py:501
  50.3 16.6 %collective-permute-start.6 = (f32[5,128,128]{2,1,0:T(8,128)}, f32[5,128,128]{2,1,0:T(8,128)}, u32[]{:S(2)}, u32[]{:S(2)}) collective-permute-start(f32[5,128,128]{2,1,0:T(8,128)} %collective-permute-done.3.refs_5_), channel_id=1, source_target_pairs={{0,1},{1,0},{2,3},{3,2},{4,5},{5,4},{6,7},{7,6},{8,9},{9,8},{10,11... | collective-permute-start | bytes 983048 | tf_op jit(solution)/shard_map/ppermute | solution.py:498
  50.3 16.1 %collective-permute-start.9 = (f32[3,128,128]{2,1,0:T(8,128)}, f32[3,128,128]{2,1,0:T(8,128)S(1)}, u32[]{:S(2)}, u32[]{:S(2)}) collective-permute-start(f32[3,128,128]{2,1,0:T(8,128)} %get-tuple-element.34), channel_id=1, source_target_pairs={{0,6},{1,27},{2,8},{3,29},{4,10},{5,31},{6,12},{7,1},{8,14},{9,3},... | collective-permute-start | bytes 589832 | tf_op jit(solution)/shard_map/ppermute | solution.py:501
  54.3 29.8 %copy-start.2 = (f32[6,128,128]{2,1,0:T(8,128)}, f32[6,128,128]{2,1,0:T(8,128)S(1)}, u32[]{:S(2)}) copy-start(f32[6,128,128]{2,1,0:T(8,128)S(1)} %collective-permute-done.7.refs_7_) | copy-start | bytes 1179652
  54.3 29.8 %collective-permute-start.10 = (f32[6,128,128]{2,1,0:T(8,128)S(1)}, f32[6,128,128]{2,1,0:T(8,128)S(1)}, u32[]{:S(2)}, u32[]{:S(2)}) collective-permute-start(f32[6,128,128]{2,1,0:T(8,128)S(1)} %collective-permute-done.7.refs_7_), channel_id=1, source_target_pairs={{0,1},{1,0},{2,3},{3,2},{4,5},{5,4},{6,7},{7,6},{8,9},{9,8},{10,11... | collective-permute-start | bytes 1179656 | tf_op jit(solution)/shard_map/ppermute | solution.py:498
  66.3 17.8 %copy-start.3 = (f32[6,128,128]{2,1,0:T(8,128)}, f32[6,128,128]{2,1,0:T(8,128)S(1)}, u32[]{:S(2)}) copy-start(f32[6,128,128]{2,1,0:T(8,128)S(1)} %collective-permute-done.8.refs_8_) | copy-start | bytes 1179652
  66.3 17.9 %collective-permute-start.11 = (f32[6,128,128]{2,1,0:T(8,128)S(1)}, f32[6,128,128]{2,1,0:T(8,128)S(1)}, u32[]{:S(2)}, u32[]{:S(2)}) collective-permute-start(f32[6,128,128]{2,1,0:T(8,128)S(1)} %collective-permute-done.8.refs_8_), channel_id=1, source_target_pairs={{0,1},{1,0},{2,3},{3,2},{4,5},{5,4},{6,7},{7,6},{8,9},{9,8},{10,11... | collective-permute-start | bytes 1179656 | tf_op jit(solution)/shard_map/ppermute | solution.py:498
  66.3 17.8 %copy-start.6 = (f32[3,128,128]{2,1,0:T(8,128)}, f32[3,128,128]{2,1,0:T(8,128)S(1)}, u32[]{:S(2)}) copy-start(f32[3,128,128]{2,1,0:T(8,128)S(1)} %collective-permute-done.9.refs_9_) | copy-start | bytes 589828
  66.3 17.8 %collective-permute-start.12 = (f32[3,128,128]{2,1,0:T(8,128)S(1)}, f32[3,128,128]{2,1,0:T(8,128)S(1)}, u32[]{:S(2)}, u32[]{:S(2)}) collective-permute-start(f32[3,128,128]{2,1,0:T(8,128)S(1)} %collective-permute-done.9.refs_9_), channel_id=1, source_target_pairs={{0,1},{1,0},{2,3},{3,2},{4,5},{5,4},{6,7},{7,6},{8,9},{9,8},{10,11... | collective-permute-start | bytes 589832 | tf_op jit(solution)/shard_map/ppermute | solution.py:498
  66.8 0.8 copy-start.10
  84.1 0.7 copy-start.7
  84.2 0.8 copy-start.4
  84.2 0.9 copy-start.5

commit v2 on v1

--- a/solution.py
+++ b/solution.py
@@ -443,15 +443,18 @@
             y_low[here] = low_part
     for copy in copies[:4]:
         copy.wait()
+    extras = []
+    for side in range(2):
+        extra = dot(a_high[side], y_high[side]) + dot(a_high[side], y_low[side])
+        extras.append(extra + dot(a_low[side], y_high[side]))
+    changes = []
     for side in range(2):
         sign = -1 if side == 0 else 1
-        extra = dot(a_high[side], y_high[side]) + dot(a_high[side], y_low[side])
-        extra = extra + dot(a_low[side], y_high[side])
         bands = []
         for k in range(1, BAND + 1):
             parts = []
             for e in range(1, BAND + 1):
-                part = extra[(k - 1) * tile : k * tile, (e - 1) * tile : e * tile]
+                part = extras[side][(k - 1) * tile : k * tile, (e - 1) * tile : e * tile]
                 if k != e:
                     row = first - k if side == 0 else first + count + k - 1
                     part = jnp.where(rows.tile_at(row, sign * (e - k)) > 0, part, 0.0)
@@ -459,16 +462,15 @@
             bands.append(jnp.concatenate(parts, axis=1))
         extra_high, extra_low = split(jnp.concatenate(bands, axis=0))
         change = dot(b_high[side], extra_high) + dot(b_high[side], extra_low)
-        change = change + dot(b_low[side], extra_high)
-        for at, (of, i, e, present, place) in enumerate(targets):
-            if of == side:
-                part = change[i * tile : (i + 1) * tile, (e - 1) * tile : e * tile]
-
-                @pl.when(present)
-                def update():
-                    pltpu.make_async_copy(estimate.at[place], changed.at[at], row_sems.at[at]).wait()
-                    changed[at] -= part
-                    pltpu.make_async_copy(changed.at[at], out.at[place], row_sems.at[at]).start()
+        changes.append(change + dot(b_low[side], extra_high))
+    for at, (side, i, e, present, place) in enumerate(targets):
+        part = changes[side][i * tile : (i + 1) * tile, (e - 1) * tile : e * tile]
+
+        @pl.when(present)
+        def update():
+            pltpu.make_async_copy(estimate.at[place], changed.at[at], row_sems.at[at]).wait()
+            changed[at] -= part
+            pltpu.make_async_copy(changed.at[at], out.at[place], row_sems.at[at]).start()
 
     for at, (side, i, e, present, place) in enumerate(targets):
 
@@ -488,7 +490,7 @@
     own = coupling.reshape(held, tile, tile)
     listed = range(devices)
     smem = pl.BlockSpec(memory_space=pltpu.SMEM)
-    hbm = pl.BlockSpec(memory_space=pltpu.HBM)
+    hbm = pl.BlockSpec(memory_space=pl.ANY)
     vmem = pl.BlockSpec(memory_space=pltpu.VMEM)
 
     def blocks(count, dtype=jnp.float32):
@@ -501,17 +503,19 @@
         return lax.ppermute(value, "rows", [(i, (i + (-step if i % GROUP else step)) % devices) for i in listed])
 
     other = partner(own)
-    starts = group_starts(row_slots, slot_count, devices, own_index)
-    last = starts[SHIFTS + 1] - 1 - starts[2 * SHIFTS + 2]
+    mine = (row_slots >= own_index * slot_count) & (row_slots < (own_index + 1) * slot_count)
+    last = jnp.sum(mine.astype(jnp.int32)) - 1
     edge_row = jnp.where(own_index % GROUP == 0, 0, last) * row_tiles
     edge_out = lax.dynamic_slice_in_dim(own, edge_row, row_tiles, 0)
     edge = along(edge_out, -1)
+    starts = group_starts(lax.optimization_barrier((row_slots, edge_out))[0], slot_count, devices, own_index)
     near_out, next_out = pl.pallas_call(
         lambda *refs: near_pack_kernel(row_tiles, slot_count, *refs),
         out_shape=[blocks((BAND - 1) * row_tiles), blocks(row_tiles)],
         in_specs=[smem] + [hbm] * 2,
         out_specs=[vmem] * 2,
         scratch_shapes=[pltpu.SemaphoreType.DMA((BAND,))],
+        compiler_params=pltpu.CompilerParams(vmem_limit_bytes=4 * 2**20),
         name="near_pack",
     )(starts, own, other)
     near_rows = along(near_out, GROUP)
@@ -526,6 +530,7 @@
             pltpu.VMEM((GROUP * held, tile, tile), jnp.float32),
             pltpu.SemaphoreType.DMA((2,)),
         ],
+        compiler_params=pltpu.CompilerParams(vmem_limit_bytes=8 * 2**20),
         name="far_pack",
     )(table, own, other)
     passed = []
@@ -559,6 +564,7 @@
             pltpu.SemaphoreType.DMA((near + 2 * BAND,)),
         ],
         cost_estimate=pl.CostEstimate(flops=4 * 10**9, bytes_accessed=10**7, transcendentals=0),
+        compiler_params=pltpu.CompilerParams(vmem_limit_bytes=30 * 2**20),
         name="near_rows",
     )(table, own, other, edge, near_rows, next_rows, *passed)
     far_passed = []
@@ -581,6 +587,7 @@
             pltpu.SemaphoreType.DMA((targets,)),
         ],
         input_output_aliases={1: 0},
+        compiler_params=pltpu.CompilerParams(vmem_limit_bytes=12 * 2**20),
         name="far_rows",
     )(table, estimate, *shares, *far_in, *far_passed)
     return out.reshape(coupling.shape)

time: 92.6 us -> 84 us (0.907)
  Pallas kernels: 29.9 us -> 23.3 us
    pallas_call x1, Pallas kernels: 3.51 us -> 0.99 us  [estimate_rows(): pl.pallas_call(lambda *refs: far_pack_kernel(row_tiles, slot_count, *refs...]
    pallas_call x1, Pallas kernels: 2.83 us -> 0.92 us  [estimate_rows(): pl.pallas_call(lambda *refs: near_pack_kernel(row_tiles, slot_count, *ref...]
    reduce_sum x0 -> x1, other arithmetic: none -> 1.33 us  [estimate_rows(): last = jnp.sum(mine.astype(jnp.int32)) - 1]
    pallas_call x1, Pallas kernels: 7.14 us -> 5.9 us  [estimate_rows(): pl.pallas_call(lambda *refs: far_kernel(row_tiles, slot_count, *refs), ou...]
    unnamed x23 -> x11, local copies, waits for them, and re-layouts: 3.62 us -> 3.66 us
  transfers between devices with their start and end apart: 13 -> 13, of which waited for: 4 -> 4; matrix products, arithmetic and copies ran while one was open for 8% -> 8% of each run, Pallas kernels for 25% -> 21%
where the time goes in v2:
time: 84 us; the launch traced here: 83.7 us
  starting transfers between devices  24.8 us (30%)
  waiting for transfers between devices  24.6 us (29%)
  Pallas kernels  23.3 us (28%)
  local copies, waits for them, and re-layouts  6.91 us (8%)
  other arithmetic  2.72 us (3%)
  between operations  1.43 us (2%)
    ppermute x6, waiting for transfers between devices, along(): lax.ppermute(value, 'rows', [(i, (i + (-step if i % GROUP else step)) % d...  24.6 us
    pallas_call x1, Pallas kernels, estimate_rows(): pl.pallas_call(lambda *refs: near_kernel(row_tiles, slot_count, *refs), o...  15.5 us
    ppermute x6, starting transfers between devices, along(): lax.ppermute(value, 'rows', [(i, (i + (-step if i % GROUP else step)) % d...  14.9 us
    ppermute x7, starting transfers between devices, partner(): return lax.ppermute(value, 'rows', [(i, i ^ 1) for i in listed])  9.9 us
    pallas_call x1, Pallas kernels, estimate_rows(): pl.pallas_call(lambda *refs: far_kernel(row_tiles, slot_count, *refs), ou...  5.9 us
    unnamed x11, local copies, waits for them, and re-layouts  3.66 us
  transfers between devices with their start and end apart: 13, of which 4 were waited for; matrix products, arithmetic and copies ran while one was open for 8% of the time, Pallas kernels for 21%

profile of v2, /device:TPU:1, one launch (start us, length us, event | category | flops | bytes accessed | tf_op | source)
XLA Modules:
  0.0 83.7 jit_solution(12374672539771778731)
XLA Ops:
  0.0 0.0 collective-permute-start
  0.0 1.3 %fusion = s32[]{:T(128)} fusion(s32[64]{0:T(128)} %param.5, s32[]{:T(128)S(6)} %mul.34, s32[]{:T(128)S(6)} %mul.33), kind=kLoop, calls=%fused_computation.29 | loop fusion | flops 319 | bytes 268 | tf_op jit(solution)/shard_map/reduce_sum | solution.py:507
  2.0 1.0 %constant_dynamic-slice_fusion = f32[5,128,128]{2,1,0:T(8,128)S(1)} fusion(f32[20,128,128]{2,1,0:T(8,128)} %bitcast.14, s32[]{:T(128)S(6)} %select_n.162), kind=kLoop, calls=%fused_computation.41 | loop fusion | bytes 655364 | tf_op jit(solution)/shard_map/dynamic_slice | solution.py:509
  3.0 2.6 %collective-permute-start.1 = (f32[5,128,128]{2,1,0:T(8,128)S(1)}, f32[5,128,128]{2,1,0:T(8,128)}, u32[]{:S(2)}, u32[]{:S(2)}) collective-permute-start(f32[5,128,128]{2,1,0:T(8,128)S(1)} %constant_dynamic-slice_fusion), channel_id=1, source_target_pairs={{0,31},{1,2},{2,1},{3,4},{4,3},{5,6},{6,5},{7,8},{8,7},{9,10},{10,... | collective-permute-start | bytes 983048 | tf_op jit(solution)/shard_map/ppermute | solution.py:503
  5.6 0.8 copy.7
  6.5 0.1 add_multiply_fusion
  6.5 0.8 convert_reduce_fusion
  7.4 0.1 fusion.3
  7.5 0.0 copy-start.4
  7.5 0.1 pad_add_fusion.1.refs_0_
  7.5 5.9 %collective-permute-done.1.refs_3_ = f32[5,128,128]{2,1,0:T(8,128)} collective-permute-done((f32[5,128,128]{2,1,0:T(8,128)S(1)}, f32[5,128,128]{2,1,0:T(8,128)}, u32[]{:S(2)}, u32[]{:S(2)}) %collective-permute-start.1) | collective-permute-done | bytes 327712 | tf_op jit(solution)/shard_map/ppermute | solution.py:503
  13.4 1.7 %collective-permute-start.4 = (f32[5,128,128]{2,1,0:T(8,128)}, f32[5,128,128]{2,1,0:T(8,128)}, u32[]{:S(2)}, u32[]{:S(2)}) collective-permute-start(f32[5,128,128]{2,1,0:T(8,128)} %collective-permute-done.1.refs_3_), channel_id=1, source_target_pairs={{0,1},{1,0},{2,3},{3,2},{4,5},{5,4},{6,7},{7,6},{8,9},{9,8},{10,11... | collective-permute-start | bytes 983048 | tf_op jit(solution)/shard_map/ppermute | solution.py:500
  15.1 0.0 collective-permute-done.refs_2_
  15.1 0.0 copy-start
  15.1 1.3 %copy-done = f32[4,5,128,128]{3,2,1,0:T(8,128)S(1)} copy-done((f32[4,5,128,128]{3,2,1,0:T(8,128)S(1)}, f32[4,5,128,128]{3,2,1,0:T(8,128)}, u32[]{:S(2)}) %copy-start) | copy-done | bytes 1310744
  16.4 0.0 copy-start.1
  16.4 0.9 %near_pack.1 = (f32[10,128,128]{2,1,0:T(8,128)S(1)}, f32[5,128,128]{2,1,0:T(8,128)S(1)}) custom-call(s32[10]{0:T(128)S(1)} %pad_add_fusion.1.refs_0_, f32[20,128,128]{2,1,0:T(8,128)S(1)} %bitcast.15, f32[20,128,128]{2,1,0:T(8,128)S(1)} %collective-permute-done.refs_2_), custom_call_target="tpu_custom_call" | custom-call | tf_op jit(solution)/shard_map/near_pack/pallas_call | solution.py:512
  17.4 0.0 copy-start.2
  17.4 0.8 copy-done.2
  18.2 0.0 copy-start.3
  18.2 0.7 copy-done.3
  18.9 0.6 slice.3
  20.2 0.0 copy-done.4
  20.2 0.7 gather_fusion
  20.9 4.9 %collective-permute-start.2 = (f32[10,128,128]{2,1,0:T(8,128)}, f32[10,128,128]{2,1,0:T(8,128)S(1)}, u32[]{:S(2)}, u32[]{:S(2)}) collective-permute-start(f32[10,128,128]{2,1,0:T(8,128)} %copy-done.2), channel_id=1, source_target_pairs={{0,2},{1,31},{2,4},{3,1},{4,6},{5,3},{6,8},{7,5},{8,10},{9,7},{10,... | collective-permute-start | bytes 1966088 | tf_op jit(solution)/shard_map/ppermute | solution.py:503
  25.8 0.6 gather_fusion.1
  26.4 0.1 compare_select_fusion
  26.5 0.1 copy.8
  26.6 0.1 sub.63
  26.7 0.5 collective-permute-start.3
  27.1 0.1 select_reduce_fusion
  27.2 9.2 %collective-permute-done.2.refs_4_ = f32[10,128,128]{2,1,0:T(8,128)S(1)} collective-permute-done((f32[10,128,128]{2,1,0:T(8,128)}, f32[10,128,128]{2,1,0:T(8,128)S(1)}, u32[]{:S(2)}, u32[]{:S(2)}) %collective-permute-start.2) | collective-permute-done | bytes 655392 | tf_op jit(solution)/shard_map/ppermute | solution.py:503
  36.4 2.7 %collective-permute-start.5 = (f32[10,128,128]{2,1,0:T(8,128)S(1)}, f32[10,128,128]{2,1,0:T(8,128)}, u32[]{:S(2)}, u32[]{:S(2)}) collective-permute-start(f32[10,128,128]{2,1,0:T(8,128)S(1)} %collective-permute-done.2.refs_4_), channel_id=1, source_target_pairs={{0,1},{1,0},{2,3},{3,2},{4,5},{5,4},{6,7},{7,6},{8,9},{9,8},{10,11... | collective-permute-start | bytes 1966088 | tf_op jit(solution)/shard_map/ppermute | solution.py:500
  39.1 0.1 copy.9
  39.2 0.1 sub.67
  39.3 0.1 pad_add_fusion.refs_0_
  39.4 0.0 copy-done.1
  39.4 1.0 %far_pack.1 = (f32[6,128,128]{2,1,0:T(8,128)S(1)}, f32[6,128,128]{2,1,0:T(8,128)S(1)}, f32[3,128,128]{2,1,0:T(8,128)S(1)}) custom-call(s32[250]{0:T(256)S(1)} %pad_add_fusion.refs_0_, f32[20,128,128]{2,1,0:T(8,128)S(1)} %bitcast.16, f32[20,128,128]{2,1,0:T(8,128)S(1)} %collective-permute-done.refs_2_), custom_call_target="tpu_custom_call" | custom-call | tf_op jit(solution)/shard_map/far_pack/pallas_call | solution.py:524
  40.4 4.3 %collective-permute-start.7 = (f32[6,128,128]{2,1,0:T(8,128)S(1)}, f32[6,128,128]{2,1,0:T(8,128)S(1)}, u32[]{:S(2)}, u32[]{:S(2)}) collective-permute-start(f32[6,128,128]{2,1,0:T(8,128)S(1)} %get-tuple-element.34), channel_id=1, source_target_pairs={{0,2},{1,31},{2,4},{3,1},{4,6},{5,3},{6,8},{7,5},{8,10},{9,7},{10,... | collective-permute-start | bytes 1179656 | tf_op jit(solution)/shard_map/ppermute | solution.py:503
  44.6 1.2 %collective-permute-start.8 = (f32[6,128,128]{2,1,0:T(8,128)S(1)}, f32[6,128,128]{2,1,0:T(8,128)S(1)}, u32[]{:S(2)}, u32[]{:S(2)}) collective-permute-start(f32[6,128,128]{2,1,0:T(8,128)S(1)} %get-tuple-element.35), channel_id=1, source_target_pairs={{0,4},{1,29},{2,6},{3,31},{4,8},{5,1},{6,10},{7,3},{8,12},{9,5},{1... | collective-permute-start | bytes 1179656 | tf_op jit(solution)/shard_map/ppermute | solution.py:503
  45.9 0.0 collective-permute-done.3.refs_5_
  45.9 0.0 collective-permute-start.6
  45.9 0.0 collective-permute-done.4.refs_6_
  45.9 1.3 %collective-permute-start.9 = (f32[3,128,128]{2,1,0:T(8,128)S(1)}, f32[3,128,128]{2,1,0:T(8,128)S(1)}, u32[]{:S(2)}, u32[]{:S(2)}) collective-permute-start(f32[3,128,128]{2,1,0:T(8,128)S(1)} %get-tuple-element.36), channel_id=1, source_target_pairs={{0,6},{1,27},{2,8},{3,29},{4,10},{5,31},{6,12},{7,1},{8,14},{9,3},... | collective-permute-start | bytes 589832 | tf_op jit(solution)/shard_map/ppermute | solution.py:503
  47.3 2.4 %collective-permute-done.7.refs_7_ = f32[6,128,128]{2,1,0:T(8,128)S(1)} collective-permute-done((f32[6,128,128]{2,1,0:T(8,128)S(1)}, f32[6,128,128]{2,1,0:T(8,128)S(1)}, u32[]{:S(2)}, u32[]{:S(2)}) %collective-permute-start.7) | collective-permute-done | bytes 393248 | tf_op jit(solution)/shard_map/ppermute | solution.py:503
  49.7 5.0 %collective-permute-start.10 = (f32[6,128,128]{2,1,0:T(8,128)S(1)}, f32[6,128,128]{2,1,0:T(8,128)S(1)}, u32[]{:S(2)}, u32[]{:S(2)}) collective-permute-start(f32[6,128,128]{2,1,0:T(8,128)S(1)} %collective-permute-done.7.refs_7_), channel_id=1, source_target_pairs={{0,1},{1,0},{2,3},{3,2},{4,5},{5,4},{6,7},{7,6},{8,9},{9,8},{10,11... | collective-permute-start | bytes 1179656 | tf_op jit(solution)/shard_map/ppermute | solution.py:500
  54.6 7.1 %collective-permute-done.8.refs_8_ = f32[6,128,128]{2,1,0:T(8,128)S(1)} collective-permute-done((f32[6,128,128]{2,1,0:T(8,128)S(1)}, f32[6,128,128]{2,1,0:T(8,128)S(1)}, u32[]{:S(2)}, u32[]{:S(2)}) %collective-permute-start.8) | collective-permute-done | bytes 393248 | tf_op jit(solution)/shard_map/ppermute | solution.py:503
  61.8 0.0 collective-permute-start.11
  61.8 0.0 collective-permute-done.9.refs_9_
  61.8 0.5 collective-permute-start.12
  62.3 0.0 collective-permute-done.6.refs_8_
  62.3 0.0 collective-permute-done.5.refs_7_
  62.3 15.5 %near_rows.1 = (f32[20,128,128]{2,1,0:T(8,128)}, bf16[2,384,384]{2,1,0:T(8,128)(2,1)S(1)}, bf16[2,384,384]{2,1,0:T(8,128)(2,1)S(1)}, bf16[2,384,384]{2,1,0:T(8,1...) custom-call(s32[250]{0:T(256)S(1)} %pad_add_fusion.refs_0_, f32[20,128,128]{2,1,0:T(8,128)S(1)} %bitcast.17, ...), custom_call_target="tpu_custom_call" | custom-call | flops 4000000000 | bytes 10000000 | tf_op jit(solution)/shard_map/near_rows/pallas_call | solution.py:546
  77.8 0.0 collective-permute-done.12.refs_12_
  77.8 0.0 collective-permute-done.10.refs_10_
  77.8 0.0 collective-permute-done.11.refs_11_
  77.8 5.9 %far_rows.1 = f32[20,128,128]{2,1,0:T(8,128)} custom-call(s32[250]{0:T(256)S(1)} %pad_add_fusion.refs_0_, f32[20,128,128]{2,1,0:T(8,128)} %get-tuple-element.25.refs_1_, bf16[2,384,384]{2,1,0:T(8,128)(2,1)S(1)} %get-tuple-element.26.refs_2_, bf16[2,384,384]{2,1,0:T(8,128)(2,1)S(1)} %get-tuple-element.27.refs_3_, ...), custom_call_target="tpu_custom_call", output_to_operand_aliasing={{}: (1, {})} | custom-call | tf_op jit(solution)/shard_map/far_rows/pallas_call | solution.py:574
  (11 shorter events, 0.1 us)
Async XLA Ops:
  0.0 15.1 %collective-permute-start = (f32[20,128,128]{2,1,0:T(8,128)}, f32[20,128,128]{2,1,0:T(8,128)S(1)}, u32[]{:S(2)}, u32[]{:S(2)}) collective-permute-start(f32[20,128,128]{2,1,0:T(8,128)} %bitcast.13), channel_id=1, source_target_pairs={{0,1},{1,0},{2,3},{3,2},{4,5},{5,4},{6,7},{7,6},{8,9},{9,8},{10,11... | collective-permute-start | bytes 3932168 | tf_op jit(solution)/shard_map/ppermute | solution.py:500
  3.0 10.4 %collective-permute-start.1 = (f32[5,128,128]{2,1,0:T(8,128)S(1)}, f32[5,128,128]{2,1,0:T(8,128)}, u32[]{:S(2)}, u32[]{:S(2)}) collective-permute-start(f32[5,128,128]{2,1,0:T(8,128)S(1)} %constant_dynamic-slice_fusion), channel_id=1, source_target_pairs={{0,31},{1,2},{2,1},{3,4},{4,3},{5,6},{6,5},{7,8},{8,7},{9,10},{10,... | collective-permute-start | bytes 983048 | tf_op jit(solution)/shard_map/ppermute | solution.py:503
  7.5 12.7 %copy-start.4 = (s32[64]{0:T(128)S(1)}, s32[64]{0:T(128)}, u32[]{:S(2)}) copy-start(s32[64]{0:T(128)} %param.5) | copy-start | bytes 772
  13.4 32.5 %collective-permute-start.4 = (f32[5,128,128]{2,1,0:T(8,128)}, f32[5,128,128]{2,1,0:T(8,128)}, u32[]{:S(2)}, u32[]{:S(2)}) collective-permute-start(f32[5,128,128]{2,1,0:T(8,128)} %collective-permute-done.1.refs_3_), channel_id=1, source_target_pairs={{0,1},{1,0},{2,3},{3,2},{4,5},{5,4},{6,7},{7,6},{8,9},{9,8},{10,11... | collective-permute-start | bytes 983048 | tf_op jit(solution)/shard_map/ppermute | solution.py:500
  15.1 1.3 %copy-start = (f32[4,5,128,128]{3,2,1,0:T(8,128)S(1)}, f32[4,5,128,128]{3,2,1,0:T(8,128)}, u32[]{:S(2)}) copy-start(f32[4,5,128,128]{3,2,1,0:T(8,128)} %param.3) | copy-start | bytes 3932164
  16.4 23.0 %copy-start.1 = (f32[4,5,128,128]{3,2,1,0:T(8,128)S(1)}, f32[4,5,128,128]{3,2,1,0:T(8,128)}, u32[]{:S(2)}) copy-start(f32[4,5,128,128]{3,2,1,0:T(8,128)} %param.3) | copy-start | bytes 3932164
  17.4 0.8 %copy-start.2 = (f32[10,128,128]{2,1,0:T(8,128)}, f32[10,128,128]{2,1,0:T(8,128)S(1)}, u32[]{:S(2)}) copy-start(f32[10,128,128]{2,1,0:T(8,128)S(1)} %get-tuple-element.22) | copy-start | bytes 1966084
  18.2 0.7 copy-start.3
  20.9 15.5 %collective-permute-start.2 = (f32[10,128,128]{2,1,0:T(8,128)}, f32[10,128,128]{2,1,0:T(8,128)S(1)}, u32[]{:S(2)}, u32[]{:S(2)}) collective-permute-start(f32[10,128,128]{2,1,0:T(8,128)} %copy-done.2), channel_id=1, source_target_pairs={{0,2},{1,31},{2,4},{3,1},{4,6},{5,3},{6,8},{7,5},{8,10},{9,7},{10,... | collective-permute-start | bytes 1966088 | tf_op jit(solution)/shard_map/ppermute | solution.py:503
  26.7 19.2 %collective-permute-start.3 = (f32[5,128,128]{2,1,0:T(8,128)}, f32[5,128,128]{2,1,0:T(8,128)}, u32[]{:S(2)}, u32[]{:S(2)}) collective-permute-start(f32[5,128,128]{2,1,0:T(8,128)} %copy-done.3), channel_id=1, source_target_pairs={{0,4},{1,29},{2,6},{3,31},{4,8},{5,1},{6,10},{7,3},{8,12},{9,5},{1... | collective-permute-start | bytes 983048 | tf_op jit(solution)/shard_map/ppermute | solution.py:503
  36.4 25.9 %collective-permute-start.5 = (f32[10,128,128]{2,1,0:T(8,128)S(1)}, f32[10,128,128]{2,1,0:T(8,128)}, u32[]{:S(2)}, u32[]{:S(2)}) collective-permute-start(f32[10,128,128]{2,1,0:T(8,128)S(1)} %collective-permute-done.2.refs_4_), channel_id=1, source_target_pairs={{0,1},{1,0},{2,3},{3,2},{4,5},{5,4},{6,7},{7,6},{8,9},{9,8},{10,11... | collective-permute-start | bytes 1966088 | tf_op jit(solution)/shard_map/ppermute | solution.py:500
  40.4 9.3 %collective-permute-start.7 = (f32[6,128,128]{2,1,0:T(8,128)S(1)}, f32[6,128,128]{2,1,0:T(8,128)S(1)}, u32[]{:S(2)}, u32[]{:S(2)}) collective-permute-start(f32[6,128,128]{2,1,0:T(8,128)S(1)} %get-tuple-element.34), channel_id=1, source_target_pairs={{0,2},{1,31},{2,4},{3,1},{4,6},{5,3},{6,8},{7,5},{8,10},{9,7},{10,... | collective-permute-start | bytes 1179656 | tf_op jit(solution)/shard_map/ppermute | solution.py:503
  44.6 17.1 %collective-permute-start.8 = (f32[6,128,128]{2,1,0:T(8,128)S(1)}, f32[6,128,128]{2,1,0:T(8,128)S(1)}, u32[]{:S(2)}, u32[]{:S(2)}) collective-permute-start(f32[6,128,128]{2,1,0:T(8,128)S(1)} %get-tuple-element.35), channel_id=1, source_target_pairs={{0,4},{1,29},{2,6},{3,31},{4,8},{5,1},{6,10},{7,3},{8,12},{9,5},{1... | collective-permute-start | bytes 1179656 | tf_op jit(solution)/shard_map/ppermute | solution.py:503
  45.9 16.4 %collective-permute-start.6 = (f32[5,128,128]{2,1,0:T(8,128)}, f32[5,128,128]{2,1,0:T(8,128)S(1)}, u32[]{:S(2)}, u32[]{:S(2)}) collective-permute-start(f32[5,128,128]{2,1,0:T(8,128)} %collective-permute-done.3.refs_5_), channel_id=1, source_target_pairs={{0,1},{1,0},{2,3},{3,2},{4,5},{5,4},{6,7},{7,6},{8,9},{9,8},{10,11... | collective-permute-start | bytes 983048 | tf_op jit(solution)/shard_map/ppermute | solution.py:500
  45.9 15.9 %collective-permute-start.9 = (f32[3,128,128]{2,1,0:T(8,128)S(1)}, f32[3,128,128]{2,1,0:T(8,128)S(1)}, u32[]{:S(2)}, u32[]{:S(2)}) collective-permute-start(f32[3,128,128]{2,1,0:T(8,128)S(1)} %get-tuple-element.36), channel_id=1, source_target_pairs={{0,6},{1,27},{2,8},{3,29},{4,10},{5,31},{6,12},{7,1},{8,14},{9,3},... | collective-permute-start | bytes 589832 | tf_op jit(solution)/shard_map/ppermute | solution.py:503
  49.7 28.2 %collective-permute-start.10 = (f32[6,128,128]{2,1,0:T(8,128)S(1)}, f32[6,128,128]{2,1,0:T(8,128)S(1)}, u32[]{:S(2)}, u32[]{:S(2)}) collective-permute-start(f32[6,128,128]{2,1,0:T(8,128)S(1)} %collective-permute-done.7.refs_7_), channel_id=1, source_target_pairs={{0,1},{1,0},{2,3},{3,2},{4,5},{5,4},{6,7},{7,6},{8,9},{9,8},{10,11... | collective-permute-start | bytes 1179656 | tf_op jit(solution)/shard_map/ppermute | solution.py:500
  61.8 16.1 %collective-permute-start.11 = (f32[6,128,128]{2,1,0:T(8,128)S(1)}, f32[6,128,128]{2,1,0:T(8,128)S(1)}, u32[]{:S(2)}, u32[]{:S(2)}) collective-permute-start(f32[6,128,128]{2,1,0:T(8,128)S(1)} %collective-permute-done.8.refs_8_), channel_id=1, source_target_pairs={{0,1},{1,0},{2,3},{3,2},{4,5},{5,4},{6,7},{7,6},{8,9},{9,8},{10,11... | collective-permute-start | bytes 1179656 | tf_op jit(solution)/shard_map/ppermute | solution.py:500
  61.8 16.1 %collective-permute-start.12 = (f32[3,128,128]{2,1,0:T(8,128)S(1)}, f32[3,128,128]{2,1,0:T(8,128)S(1)}, u32[]{:S(2)}, u32[]{:S(2)}) collective-permute-start(f32[3,128,128]{2,1,0:T(8,128)S(1)} %collective-permute-done.9.refs_9_), channel_id=1, source_target_pairs={{0,1},{1,0},{2,3},{3,2},{4,5},{5,4},{6,7},{7,6},{8,9},{9,8},{10,11... | collective-permute-start | bytes 589832 | tf_op jit(solution)/shard_map/ppermute | solution.py:500

commit v3 on v2

--- a/solution.py
+++ b/solution.py
@@ -105,7 +105,7 @@
     forward = rows.core == 0
     held = slot_count * row_tiles
     wanted = []
-    for shift, ref, distances in ((1, near, range(2, BAND + 1)), (2, next_near, (BAND,))):
+    for shift, ref, distances in ((1, near, range(1, BAND + 1)), (2, next_near, (BAND,))):
         for i, d in enumerate(distances):
             edge = rows.edge(shift, forward)
             base = rows.group_tile(jnp.where(forward, edge - d, edge + d - 1))
@@ -159,8 +159,8 @@
     return jnp.dot(a, b, preferred_element_type=jnp.float32)
 
 
-def near_kernel(row_tiles, slot_count, starts, own, other, edge, near_rows, next_rows,
-                edge_p, near_p, next_p, out, a_high, a_low, b_high, b_low, inv_out,
+def near_kernel(row_tiles, slot_count, starts, own, other, near_rows, next_rows,
+                near_p, next_p, out, a_high, a_low, b_high, b_low, inv_out,
                 pool, left_high, left_low, y_high, y_low, p_high, p_low,
                 inv_row, offsets, y_at, p_at, whole, sems):
     core = starts[2 * SHIFTS + 3]
@@ -196,10 +196,9 @@
         slot = jnp.where(row < rows.middle, row - low, row - rows.middle)
         whole[w] = jnp.where(inside | (d <= BAND), 1, 0)
         choices = [(home, own, slot), (inside & jnp.logical_not(home), other, slot)]
-        for side, refs in ((mine, (edge, near_rows, next_rows)), (theirs, (edge_p, near_p, next_p))):
-            choices.append((side & (d == 1), refs[0], 0))
-            choices.append((side & (d > 1) & (d <= BAND) & (d <= reached), refs[1], d - 2))
-            choices.append((side & (d == BAND) & (d > reached), refs[2], 0))
+        for side, refs in ((mine, (near_rows, next_rows)), (theirs, (near_p, next_p))):
+            choices.append((side & (d <= BAND) & (d <= reached), refs[0], d - 1))
+            choices.append((side & (d == BAND) & (d > reached), refs[1], 0))
         for chosen, ref, at in choices:
 
             @pl.when(chosen)
@@ -313,7 +312,8 @@
                 return jnp.concatenate(lines, axis=0)
 
             high_right = right(high_ref)
-            value = dot(left_h, high_right) + dot(left_l, high_right) + dot(left_h, right(low_ref))
+            rights = jnp.concatenate([high_right, high_right, right(low_ref)], axis=0)
+            value = dot(jnp.concatenate([left_h, left_l, left_h], axis=1), rights)
             for i in range(len(pair)):
                 results.append(value[:, i * tile : (i + 1) * tile])
         return results
@@ -503,18 +503,13 @@
         return lax.ppermute(value, "rows", [(i, (i + (-step if i % GROUP else step)) % devices) for i in listed])
 
     other = partner(own)
-    mine = (row_slots >= own_index * slot_count) & (row_slots < (own_index + 1) * slot_count)
-    last = jnp.sum(mine.astype(jnp.int32)) - 1
-    edge_row = jnp.where(own_index % GROUP == 0, 0, last) * row_tiles
-    edge_out = lax.dynamic_slice_in_dim(own, edge_row, row_tiles, 0)
-    edge = along(edge_out, -1)
-    starts = group_starts(lax.optimization_barrier((row_slots, edge_out))[0], slot_count, devices, own_index)
+    starts = group_starts(row_slots, slot_count, devices, own_index)
     near_out, next_out = pl.pallas_call(
         lambda *refs: near_pack_kernel(row_tiles, slot_count, *refs),
-        out_shape=[blocks((BAND - 1) * row_tiles), blocks(row_tiles)],
+        out_shape=[blocks(BAND * row_tiles), blocks(row_tiles)],
         in_specs=[smem] + [hbm] * 2,
         out_specs=[vmem] * 2,
-        scratch_shapes=[pltpu.SemaphoreType.DMA((BAND,))],
+        scratch_shapes=[pltpu.SemaphoreType.DMA((BAND + 1,))],
         compiler_params=pltpu.CompilerParams(vmem_limit_bytes=4 * 2**20),
         name="near_pack",
     )(starts, own, other)
@@ -534,7 +529,7 @@
         name="far_pack",
     )(table, own, other)
     passed = []
-    for value in (edge, near_rows, next_rows):
+    for value in (near_rows, next_rows):
         passed.append(partner(value))
     far_out = lax.optimization_barrier((tuple(far_out), near_rows))[0]
     far_in = []
@@ -546,7 +541,7 @@
     estimate, *shares = pl.pallas_call(
         lambda *refs: near_kernel(row_tiles, slot_count, *refs),
         out_shape=[blocks(held)] + [side_block] * 4 + [jax.ShapeDtypeStruct((2 * BAND, 1, tile), jnp.float32)],
-        in_specs=[smem] + [hbm] * 8,
+        in_specs=[smem] + [hbm] * 6,
         out_specs=[vmem] * 6,
         scratch_shapes=[
             pltpu.VMEM(((near + 2 * BAND) * row_tiles, tile, tile), jnp.float32),
@@ -566,7 +561,7 @@
         cost_estimate=pl.CostEstimate(flops=4 * 10**9, bytes_accessed=10**7, transcendentals=0),
         compiler_params=pltpu.CompilerParams(vmem_limit_bytes=30 * 2**20),
         name="near_rows",
-    )(table, own, other, edge, near_rows, next_rows, *passed)
+    )(table, own, other, near_rows, next_rows, *passed)
     far_passed = []
     for shift in range(1, SHIFTS + 1):
         far_passed.append(partner(far_in[shift - 1]))

time: 84 us -> 80.7 us (0.961)
  starting transfers between devices: 24.8 us -> 30.5 us
  waiting for transfers between devices: 24.6 us -> 19.1 us
  local copies, waits for them, and re-layouts: 6.91 us -> 4.36 us
  other arithmetic: 2.72 us -> 1.4 us
  Pallas kernels: 23.3 us -> 24.3 us
    ppermute x6 -> x5, waiting for transfers between devices: 24.6 us -> 17.8 us  [along(): lax.ppermute(value, 'rows', [(i, (i + (-step if i % GROUP else step)) % d...]
    ppermute x7 -> x6, starting transfers between devices: 9.9 us -> 13 us  [partner(): return lax.ppermute(value, 'rows', [(i, i ^ 1) for i in listed])]
    ppermute x6 -> x5, starting transfers between devices: 14.9 us -> 17.5 us  [along(): lax.ppermute(value, 'rows', [(i, (i + (-step if i % GROUP else step)) % d...]
    unnamed x11 -> x7, local copies, waits for them, and re-layouts: 3.66 us -> 2.12 us
    reduce_sum x1 -> x0, other arithmetic: 1.33 us -> none  [estimate_rows(): last = jnp.sum(mine.astype(jnp.int32)) - 1]
    ppermute x7 -> x6, waiting for transfers between devices: 0.02 us -> 1.33 us  [partner(): return lax.ppermute(value, 'rows', [(i, i ^ 1) for i in listed])]
    pallas_call x1, Pallas kernels: 0.92 us -> 1.99 us  [estimate_rows(): pl.pallas_call(lambda *refs: near_pack_kernel(row_tiles, slot_count, *ref...]
    dynamic_slice x1 -> x0, local copies, waits for them, and re-layouts: 1 us -> none  [estimate_rows(): edge_out = lax.dynamic_slice_in_dim(own, edge_row, row_tiles, 0)]
  transfers between devices with their start and end apart: 13 -> 11, of which waited for: 4 -> 5; matrix products, arithmetic and copies ran while one was open for 8% -> 6% of each run, Pallas kernels for 21% -> 20%
where the time goes in v3:
time: 80.7 us; the launch traced here: 80.5 us
  starting transfers between devices  30.5 us (38%)
  Pallas kernels  24.3 us (30%)
  waiting for transfers between devices  19.1 us (24%)
  local copies, waits for them, and re-layouts  4.36 us (5%)
  other arithmetic  1.4 us (2%)
    ppermute x5, waiting for transfers between devices, along(): lax.ppermute(value, 'rows', [(i, (i + (-step if i % GROUP else step)) % d...  17.8 us
    ppermute x5, starting transfers between devices, along(): lax.ppermute(value, 'rows', [(i, (i + (-step if i % GROUP else step)) % d...  17.5 us
    pallas_call x1, Pallas kernels, estimate_rows(): pl.pallas_call(lambda *refs: near_kernel(row_tiles, slot_count, *refs), o...  15.5 us
    ppermute x6, starting transfers between devices, partner(): return lax.ppermute(value, 'rows', [(i, i ^ 1) for i in listed])  13 us
    pallas_call x1, Pallas kernels, estimate_rows(): pl.pallas_call(lambda *refs: far_kernel(row_tiles, slot_count, *refs), ou...  5.9 us
    unnamed x7, local copies, waits for them, and re-layouts  2.12 us
    pallas_call x1, Pallas kernels, estimate_rows(): pl.pallas_call(lambda *refs: near_pack_kernel(row_tiles, slot_count, *ref...  1.99 us
  transfers between devices with their start and end apart: 11, of which 5 were waited for; matrix products, arithmetic and copies ran while one was open for 6% of the time, Pallas kernels for 20%

profile of v3, /device:TPU:1, one launch (start us, length us, event | category | flops | bytes accessed | tf_op | source)
XLA Modules:
  0.0 80.5 jit_solution(8526592156379090334)
XLA Ops:
  0.0 0.0 collective-permute-start
  0.0 0.8 copy.7
  0.9 0.1 add_multiply_fusion
  0.9 0.8 %convert_reduce_fusion = s32[9]{0:T(128)S(1)} fusion(s32[64]{0:T(128)} %param.5, s32[9]{0:T(128)S(1)} %add_multiply_fusion), kind=kLoop, calls=%fused_computation.6 | loop fusion | flops 1719 | bytes 328 | tf_op jit(solution)/shard_map/reduce_sum | solution.py:31
  1.8 0.1 fusion.2
  1.8 0.1 pad_add_fusion.1.refs_0_
  1.9 1.3 %collective-permute-done.refs_2_ = f32[20,128,128]{2,1,0:T(8,128)S(1)} collective-permute-done((f32[20,128,128]{2,1,0:T(8,128)}, f32[20,128,128]{2,1,0:T(8,128)S(1)}, u32[]{:S(2)}, u32[]{:S(2)}) %collective-permute-start) | collective-permute-done | bytes 1310752 | tf_op jit(solution)/shard_map/ppermute | solution.py:500
  3.2 0.0 copy-start
  3.2 1.3 %copy-done = f32[4,5,128,128]{3,2,1,0:T(8,128)S(1)} copy-done((f32[4,5,128,128]{3,2,1,0:T(8,128)S(1)}, f32[4,5,128,128]{3,2,1,0:T(8,128)}, u32[]{:S(2)}) %copy-start) | copy-done | bytes 1310744
  4.6 0.0 copy-start.2
  4.6 0.0 copy-start.1
  4.6 2.0 %near_pack.1 = (f32[15,128,128]{2,1,0:T(8,128)}, f32[5,128,128]{2,1,0:T(8,128)S(1)}) custom-call(s32[10]{0:T(128)S(1)} %pad_add_fusion.1.refs_0_, f32[20,128,128]{2,1,0:T(8,128)S(1)} %bitcast.14, f32[20,128,128]{2,1,0:T(8,128)S(1)} %collective-permute-done.refs_2_), custom_call_target="tpu_custom_call" | custom-call | tf_op jit(solution)/shard_map/near_pack/pallas_call | solution.py:507
  6.6 6.4 %collective-permute-start.1 = (f32[15,128,128]{2,1,0:T(8,128)}, f32[15,128,128]{2,1,0:T(8,128)}, u32[]{:S(2)}, u32[]{:S(2)}) collective-permute-start(f32[15,128,128]{2,1,0:T(8,128)} %get-tuple-element.20), channel_id=1, source_target_pairs={{0,2},{1,31},{2,4},{3,1},{4,6},{5,3},{6,8},{7,5},{8,10},{9,7},{10,... | collective-permute-start | bytes 2949128 | tf_op jit(solution)/shard_map/ppermute | solution.py:503
  12.9 0.6 slice.3
  14.2 0.0 copy-done.2
  14.2 0.7 gather_fusion
  14.9 0.6 gather_fusion.1
  15.5 0.1 compare_select_fusion
  15.6 0.1 copy.8
  15.7 13.5 %collective-permute-done.1.refs_3_ = f32[15,128,128]{2,1,0:T(8,128)} collective-permute-done((f32[15,128,128]{2,1,0:T(8,128)}, f32[15,128,128]{2,1,0:T(8,128)}, u32[]{:S(2)}, u32[]{:S(2)}) %collective-permute-start.1) | collective-permute-done | bytes 983072 | tf_op jit(solution)/shard_map/ppermute | solution.py:503
  29.2 2.8 %collective-permute-start.3 = (f32[15,128,128]{2,1,0:T(8,128)}, f32[15,128,128]{2,1,0:T(8,128)}, u32[]{:S(2)}, u32[]{:S(2)}) collective-permute-start(f32[15,128,128]{2,1,0:T(8,128)} %collective-permute-done.1.refs_3_), channel_id=1, source_target_pairs={{0,1},{1,0},{2,3},{3,2},{4,5},{5,4},{6,7},{7,6},{8,9},{9,8},{10,11... | collective-permute-start | bytes 2949128 | tf_op jit(solution)/shard_map/ppermute | solution.py:500
  32.1 0.1 select_reduce_fusion
  32.2 0.1 copy.9
  32.3 0.1 sub.63
  32.3 0.1 sub.59
  32.4 4.4 %collective-permute-start.2 = (f32[5,128,128]{2,1,0:T(8,128)S(1)}, f32[5,128,128]{2,1,0:T(8,128)S(1)}, u32[]{:S(2)}, u32[]{:S(2)}) collective-permute-start(f32[5,128,128]{2,1,0:T(8,128)S(1)} %get-tuple-element.22), channel_id=1, source_target_pairs={{0,4},{1,29},{2,6},{3,31},{4,8},{5,1},{6,10},{7,3},{8,12},{9,5},{1... | collective-permute-start | bytes 983048 | tf_op jit(solution)/shard_map/ppermute | solution.py:503
  36.9 0.1 pad_add_fusion.refs_0_
  37.0 0.0 copy-done.1
  37.0 1.0 %far_pack.1 = (f32[6,128,128]{2,1,0:T(8,128)S(1)}, f32[6,128,128]{2,1,0:T(8,128)S(1)}, f32[3,128,128]{2,1,0:T(8,128)S(1)}) custom-call(s32[250]{0:T(256)S(1)} %pad_add_fusion.refs_0_, f32[20,128,128]{2,1,0:T(8,128)S(1)} %bitcast.15, f32[20,128,128]{2,1,0:T(8,128)S(1)} %collective-permute-done.refs_2_), custom_call_target="tpu_custom_call" | custom-call | tf_op jit(solution)/shard_map/far_pack/pallas_call | solution.py:519
  38.0 2.1 %collective-permute-start.5 = (f32[6,128,128]{2,1,0:T(8,128)S(1)}, f32[6,128,128]{2,1,0:T(8,128)S(1)}, u32[]{:S(2)}, u32[]{:S(2)}) collective-permute-start(f32[6,128,128]{2,1,0:T(8,128)S(1)} %get-tuple-element.32), channel_id=1, source_target_pairs={{0,2},{1,31},{2,4},{3,1},{4,6},{5,3},{6,8},{7,5},{8,10},{9,7},{10,... | collective-permute-start | bytes 1179656 | tf_op jit(solution)/shard_map/ppermute | solution.py:503
  40.0 0.2 collective-permute-start.6
  40.3 1.7 %collective-permute-done.2.refs_4_ = f32[5,128,128]{2,1,0:T(8,128)S(1)} collective-permute-done((f32[5,128,128]{2,1,0:T(8,128)S(1)}, f32[5,128,128]{2,1,0:T(8,128)S(1)}, u32[]{:S(2)}, u32[]{:S(2)}) %collective-permute-start.2) | collective-permute-done | bytes 327712 | tf_op jit(solution)/shard_map/ppermute | solution.py:503
  41.9 8.6 %collective-permute-start.4 = (f32[5,128,128]{2,1,0:T(8,128)S(1)}, f32[5,128,128]{2,1,0:T(8,128)S(1)}, u32[]{:S(2)}, u32[]{:S(2)}) collective-permute-start(f32[5,128,128]{2,1,0:T(8,128)S(1)} %collective-permute-done.2.refs_4_), channel_id=1, source_target_pairs={{0,1},{1,0},{2,3},{3,2},{4,5},{5,4},{6,7},{7,6},{8,9},{9,8},{10,11... | collective-permute-start | bytes 983048 | tf_op jit(solution)/shard_map/ppermute | solution.py:500
  50.5 4.4 %collective-permute-start.7 = (f32[3,128,128]{2,1,0:T(8,128)S(1)}, f32[3,128,128]{2,1,0:T(8,128)S(1)}, u32[]{:S(2)}, u32[]{:S(2)}) collective-permute-start(f32[3,128,128]{2,1,0:T(8,128)S(1)} %get-tuple-element.34), channel_id=1, source_target_pairs={{0,6},{1,27},{2,8},{3,29},{4,10},{5,31},{6,12},{7,1},{8,14},{9,3},... | collective-permute-start | bytes 589832 | tf_op jit(solution)/shard_map/ppermute | solution.py:503
  54.9 0.0 collective-permute-done.5.refs_7_
  54.9 0.0 collective-permute-start.8
  54.9 2.4 %collective-permute-done.6.refs_8_ = f32[6,128,128]{2,1,0:T(8,128)S(1)} collective-permute-done((f32[6,128,128]{2,1,0:T(8,128)S(1)}, f32[6,128,128]{2,1,0:T(8,128)S(1)}, u32[]{:S(2)}, u32[]{:S(2)}) %collective-permute-start.6) | collective-permute-done | bytes 393248 | tf_op jit(solution)/shard_map/ppermute | solution.py:503
  57.4 0.0 collective-permute-start.9
  57.4 0.2 collective-permute-done.7.refs_9_
  57.5 1.6 %collective-permute-start.10 = (f32[3,128,128]{2,1,0:T(8,128)S(1)}, f32[3,128,128]{2,1,0:T(8,128)S(1)}, u32[]{:S(2)}, u32[]{:S(2)}) collective-permute-start(f32[3,128,128]{2,1,0:T(8,128)S(1)} %collective-permute-done.7.refs_9_), channel_id=1, source_target_pairs={{0,1},{1,0},{2,3},{3,2},{4,5},{5,4},{6,7},{7,6},{8,9},{9,8},{10,11... | collective-permute-start | bytes 589832 | tf_op jit(solution)/shard_map/ppermute | solution.py:500
  59.1 0.0 collective-permute-done.4.refs_6_
  59.1 0.0 collective-permute-done.3.refs_5_
  59.1 15.5 %near_rows.1 = (f32[20,128,128]{2,1,0:T(8,128)}, bf16[2,384,384]{2,1,0:T(8,128)(2,1)S(1)}, bf16[2,384,384]{2,1,0:T(8,128)(2,1)S(1)}, bf16[2,384,384]{2,1,0:T(8,1...) custom-call(s32[250]{0:T(256)S(1)} %pad_add_fusion.refs_0_, f32[20,128,128]{2,1,0:T(8,128)S(1)} %bitcast.16, ...), custom_call_target="tpu_custom_call" | custom-call | flops 4000000000 | bytes 10000000 | tf_op jit(solution)/shard_map/near_rows/pallas_call | solution.py:541
  74.6 0.0 collective-permute-done.10.refs_12_
  74.6 0.0 collective-permute-done.8.refs_10_
  74.6 0.0 collective-permute-done.9.refs_11_
  74.6 5.9 %far_rows.1 = f32[20,128,128]{2,1,0:T(8,128)} custom-call(s32[250]{0:T(256)S(1)} %pad_add_fusion.refs_0_, f32[20,128,128]{2,1,0:T(8,128)} %get-tuple-element.23.refs_1_, bf16[2,384,384]{2,1,0:T(8,128)(2,1)S(1)} %get-tuple-element.24.refs_2_, bf16[2,384,384]{2,1,0:T(8,128)(2,1)S(1)} %get-tuple-element.25.refs_3_, ...), custom_call_target="tpu_custom_call", output_to_operand_aliasing={{}: (1, {})} | custom-call | tf_op jit(solution)/shard_map/far_rows/pallas_call | solution.py:569
  (11 shorter events, 0.1 us)
Async XLA Ops:
  0.0 3.2 %collective-permute-start = (f32[20,128,128]{2,1,0:T(8,128)}, f32[20,128,128]{2,1,0:T(8,128)S(1)}, u32[]{:S(2)}, u32[]{:S(2)}) collective-permute-start(f32[20,128,128]{2,1,0:T(8,128)} %bitcast.13), channel_id=1, source_target_pairs={{0,1},{1,0},{2,3},{3,2},{4,5},{5,4},{6,7},{7,6},{8,9},{9,8},{10,11... | collective-permute-start | bytes 3932168 | tf_op jit(solution)/shard_map/ppermute | solution.py:500
  3.2 1.3 %copy-start = (f32[4,5,128,128]{3,2,1,0:T(8,128)S(1)}, f32[4,5,128,128]{3,2,1,0:T(8,128)}, u32[]{:S(2)}) copy-start(f32[4,5,128,128]{3,2,1,0:T(8,128)} %param.3) | copy-start | bytes 3932164
  4.6 9.6 %copy-start.2 = (s32[64]{0:T(128)S(1)}, s32[64]{0:T(128)}, u32[]{:S(2)}) copy-start(s32[64]{0:T(128)} %param.5) | copy-start | bytes 772
  4.6 32.4 %copy-start.1 = (f32[4,5,128,128]{3,2,1,0:T(8,128)S(1)}, f32[4,5,128,128]{3,2,1,0:T(8,128)}, u32[]{:S(2)}) copy-start(f32[4,5,128,128]{3,2,1,0:T(8,128)} %param.3) | copy-start | bytes 3932164
  6.6 22.7 %collective-permute-start.1 = (f32[15,128,128]{2,1,0:T(8,128)}, f32[15,128,128]{2,1,0:T(8,128)}, u32[]{:S(2)}, u32[]{:S(2)}) collective-permute-start(f32[15,128,128]{2,1,0:T(8,128)} %get-tuple-element.20), channel_id=1, source_target_pairs={{0,2},{1,31},{2,4},{3,1},{4,6},{5,3},{6,8},{7,5},{8,10},{9,7},{10,... | collective-permute-start | bytes 2949128 | tf_op jit(solution)/shard_map/ppermute | solution.py:503
  29.2 29.8 %collective-permute-start.3 = (f32[15,128,128]{2,1,0:T(8,128)}, f32[15,128,128]{2,1,0:T(8,128)}, u32[]{:S(2)}, u32[]{:S(2)}) collective-permute-start(f32[15,128,128]{2,1,0:T(8,128)} %collective-permute-done.1.refs_3_), channel_id=1, source_target_pairs={{0,1},{1,0},{2,3},{3,2},{4,5},{5,4},{6,7},{7,6},{8,9},{9,8},{10,11... | collective-permute-start | bytes 2949128 | tf_op jit(solution)/shard_map/ppermute | solution.py:500
  32.4 9.5 %collective-permute-start.2 = (f32[5,128,128]{2,1,0:T(8,128)S(1)}, f32[5,128,128]{2,1,0:T(8,128)S(1)}, u32[]{:S(2)}, u32[]{:S(2)}) collective-permute-start(f32[5,128,128]{2,1,0:T(8,128)S(1)} %get-tuple-element.22), channel_id=1, source_target_pairs={{0,4},{1,29},{2,6},{3,31},{4,8},{5,1},{6,10},{7,3},{8,12},{9,5},{1... | collective-permute-start | bytes 983048 | tf_op jit(solution)/shard_map/ppermute | solution.py:503
  38.0 17.0 %collective-permute-start.5 = (f32[6,128,128]{2,1,0:T(8,128)S(1)}, f32[6,128,128]{2,1,0:T(8,128)S(1)}, u32[]{:S(2)}, u32[]{:S(2)}) collective-permute-start(f32[6,128,128]{2,1,0:T(8,128)S(1)} %get-tuple-element.32), channel_id=1, source_target_pairs={{0,2},{1,31},{2,4},{3,1},{4,6},{5,3},{6,8},{7,5},{8,10},{9,7},{10,... | collective-permute-start | bytes 1179656 | tf_op jit(solution)/shard_map/ppermute | solution.py:503
  40.0 17.3 %collective-permute-start.6 = (f32[6,128,128]{2,1,0:T(8,128)S(1)}, f32[6,128,128]{2,1,0:T(8,128)S(1)}, u32[]{:S(2)}, u32[]{:S(2)}) collective-permute-start(f32[6,128,128]{2,1,0:T(8,128)S(1)} %get-tuple-element.33), channel_id=1, source_target_pairs={{0,4},{1,29},{2,6},{3,31},{4,8},{5,1},{6,10},{7,3},{8,12},{9,5},{1... | collective-permute-start | bytes 1179656 | tf_op jit(solution)/shard_map/ppermute | solution.py:503
  41.9 17.2 %collective-permute-start.4 = (f32[5,128,128]{2,1,0:T(8,128)S(1)}, f32[5,128,128]{2,1,0:T(8,128)S(1)}, u32[]{:S(2)}, u32[]{:S(2)}) collective-permute-start(f32[5,128,128]{2,1,0:T(8,128)S(1)} %collective-permute-done.2.refs_4_), channel_id=1, source_target_pairs={{0,1},{1,0},{2,3},{3,2},{4,5},{5,4},{6,7},{7,6},{8,9},{9,8},{10,11... | collective-permute-start | bytes 983048 | tf_op jit(solution)/shard_map/ppermute | solution.py:500
  50.5 7.0 %collective-permute-start.7 = (f32[3,128,128]{2,1,0:T(8,128)S(1)}, f32[3,128,128]{2,1,0:T(8,128)S(1)}, u32[]{:S(2)}, u32[]{:S(2)}) collective-permute-start(f32[3,128,128]{2,1,0:T(8,128)S(1)} %get-tuple-element.34), channel_id=1, source_target_pairs={{0,6},{1,27},{2,8},{3,29},{4,10},{5,31},{6,12},{7,1},{8,14},{9,3},... | collective-permute-start | bytes 589832 | tf_op jit(solution)/shard_map/ppermute | solution.py:503
  54.9 19.7 %collective-permute-start.8 = (f32[6,128,128]{2,1,0:T(8,128)S(1)}, f32[6,128,128]{2,1,0:T(8,128)S(1)}, u32[]{:S(2)}, u32[]{:S(2)}) collective-permute-start(f32[6,128,128]{2,1,0:T(8,128)S(1)} %collective-permute-done.5.refs_7_), channel_id=1, source_target_pairs={{0,1},{1,0},{2,3},{3,2},{4,5},{5,4},{6,7},{7,6},{8,9},{9,8},{10,11... | collective-permute-start | bytes 1179656 | tf_op jit(solution)/shard_map/ppermute | solution.py:500
  57.4 17.2 %collective-permute-start.9 = (f32[6,128,128]{2,1,0:T(8,128)S(1)}, f32[6,128,128]{2,1,0:T(8,128)S(1)}, u32[]{:S(2)}, u32[]{:S(2)}) collective-permute-start(f32[6,128,128]{2,1,0:T(8,128)S(1)} %collective-permute-done.6.refs_8_), channel_id=1, source_target_pairs={{0,1},{1,0},{2,3},{3,2},{4,5},{5,4},{6,7},{7,6},{8,9},{9,8},{10,11... | collective-permute-start | bytes 1179656 | tf_op jit(solution)/shard_map/ppermute | solution.py:500
  57.5 17.1 %collective-permute-start.10 = (f32[3,128,128]{2,1,0:T(8,128)S(1)}, f32[3,128,128]{2,1,0:T(8,128)S(1)}, u32[]{:S(2)}, u32[]{:S(2)}) collective-permute-start(f32[3,128,128]{2,1,0:T(8,128)S(1)} %collective-permute-done.7.refs_9_), channel_id=1, source_target_pairs={{0,1},{1,0},{2,3},{3,2},{4,5},{5,4},{6,7},{7,6},{8,9},{9,8},{10,11... | collective-permute-start | bytes 589832 | tf_op jit(solution)/shard_map/ppermute | solution.py:500
